TPU v7x, 256 devices: a whole 4x4x8 slice. The times are simulated.
256 devices in a mesh: gx: 2 (over z_lo), gy: 16 (over x, y), gz: 8 (over z_hi, core).
Axes of the slice: x: 4, y: 4, z: 8 (z_hi: 4, z_lo: 2; z = z_hi * 2 + z_lo), core: 2. Of those that a mesh axis runs over, the one named last changes fastest.
Arguments:
- factors: bfloat16 [6144, 8, 4096], P('gy', None, 'gz'), may hold values from -0.046875 to 0.046875
- trial_vectors: float32 [64, 8, 4096], P('gx', None, 'gz'), may hold values from -6 to 6
- energy_gap: float32 [8, 4096], P(None, 'gz'), may hold values from 0.5 to 4
Outputs:
- updated_vectors: float32 [64, 8, 4096], P('gx', None, 'gz')
- coupling: float32 [64, 64], P(None, 'gx')
All inputs are finite; a program needn't handle non-finite values.
Results may differ from a plain program's by a relative error of at most 0.02.
Values may be sent and summed in bfloat16 or wider, within the bound.
No kernel may reach another device: no remote copies, remote signals or barrier semaphores. Data moves between devices by JAX's collectives and lax.ppermute only.
A program may use at most 64 MiB of HBM per device.

v0:
```python
import jax
import jax.numpy as jnp
from jax import lax
from jax.experimental import pallas as pl
from jax.experimental.pallas import tpu as pltpu
from jax.sharding import PartitionSpec as P

ITERS = 2
BF = jnp.bfloat16
F32 = jnp.float32
HIGHEST = lax.Precision.HIGHEST


NT = (((1,), (1,)), ((), ()))
NN = (((1,), (0,)), ((), ()))
TN = (((0,), (0,)), ((), ()))


def dot(a, b, dims, precision=None):
    return lax.dot_general(a, b, dims, precision=precision, preferred_element_type=F32)


SMEM = pl.BlockSpec(memory_space=pltpu.SMEM)
VMEM = pl.BlockSpec(memory_space=pltpu.VMEM)
PARAMS = pltpu.CompilerParams(vmem_limit_bytes=24 << 20)


def array(shape, dtype):
    return jax.ShapeDtypeStruct(shape, dtype)


def split(value):
    high = value.astype(BF).astype(F32)
    return high, value - high


def lanes(value, parts):
    rows = value.shape[0] // parts
    return jnp.concatenate([value[i * rows : (i + 1) * rows] for i in range(parts)], axis=1)


def unlanes(value, parts):
    width = value.shape[1] // parts
    return jnp.concatenate([value[:, i * width : (i + 1) * width] for i in range(parts)], axis=0)


def rows_of(steps, place, sibling):
    chip = place >> 1
    core = (1 - (place & 1)) if sibling else (place & 1)
    way = 2 * core - 1
    return [2 * ((chip + s * way) & 3) + core for s in steps]


def mix_kernel(place, x, b, *outs, steps):
    rows = x.shape[1]
    count = len(steps)
    order = rows_of(steps, place[2], True) + rows_of(steps, place[2], False)
    chosen = jnp.concatenate([x[j] for j in order], axis=0)
    for r in range(b.shape[0]):
        part = dot(chosen, b[r], NT)
        for j in range(count):
            theirs = part[j * rows : (j + 1) * rows]
            outs[0][j, r * rows : (r + 1) * rows, :] = theirs.astype(BF)
            mine = part[(count + j) * rows : (count + j + 1) * rows]
            outs[1 + j][r * rows : (r + 1) * rows, :] = mine


def mix(place, x, b, steps):
    r, k, _ = x.shape
    shape = (r * k, b.shape[1])
    outs = [array((len(steps), *shape), BF)] + [array(shape, F32)] * len(steps)
    return pl.pallas_call(
        lambda *refs: mix_kernel(*refs, steps=steps),
        out_shape=outs,
        in_specs=[SMEM, VMEM, VMEM],
        out_specs=[VMEM] * len(outs),
        compiler_params=PARAMS,
    )(place, x, b)


def add_kernel(mine, theirs, *refs):
    *others, out = refs
    total = mine[...] + theirs[0].astype(F32)
    for other in others:
        total += other[...].astype(F32)
    out[...] = total.astype(BF)


def add(mine, theirs, index, *others):
    whole = pl.BlockSpec(mine.shape, lambda i: (0, 0))
    return pl.pallas_call(
        add_kernel,
        grid=(1,),
        out_shape=array(mine.shape, BF),
        in_specs=[whole, pl.BlockSpec((1, *mine.shape), lambda i: (index, 0, 0))]
        + [whole] * len(others),
        out_specs=whole,
        compiler_params=PARAMS,
    )(mine, theirs, *others)


def sums_kernel(place, own, other, gap, fock, message):
    r, k, _ = own.shape
    gram = jnp.zeros((2 * k, 2 * k), F32)
    scaled = jnp.zeros((2 * k, k), F32)
    projected = jnp.zeros((2 * k, k), F32)
    for i in range(r):
        both = jnp.concatenate([own[i], other[i]], axis=0)
        gram += dot(both, both, NT)
        high, low = split(own[i].astype(F32) * gap[i : i + 1, :])
        scaled += dot(both, high.astype(BF), NT) + dot(both, low.astype(BF), NT)
        projected += dot(both, fock[i * k : (i + 1) * k, :], NT)
    once = jnp.where(place[1] == 0, 1.0, 0.0)
    projected += once * scaled
    message[...] = jnp.concatenate([lanes(gram, 2), lanes(projected, 4)], axis=0)


def local_sums(place, own, other, gap, fock):
    k = own.shape[1]
    return pl.pallas_call(
        sums_kernel,
        out_shape=array((3 * k // 2, 4 * k), F32),
        in_specs=[SMEM] + [VMEM] * 4,
        out_specs=VMEM,
        compiler_params=PARAMS,
    )(place, own, other, gap, fock)


def fock_kernel(place, *refs):
    blocks = refs[:8]
    b, out, coulomb = refs[8:]
    r, k, _ = coulomb.shape
    rows = r * k
    got = (0, -1, 1, 2)
    order = rows_of(got, place[2], False) + rows_of(got, place[2], True)
    fitted = jnp.zeros((k, blocks[0].shape[1]), F32)
    for j in range(8):
        start = pl.multiple_of(order[j] * k, k)
        fitted += blocks[j][pl.ds(start, k), :].astype(F32)
    fitted = fitted.astype(BF)
    total = jnp.zeros((rows, b.shape[2]), F32)
    for j in range(8):
        both = dot(jnp.concatenate([blocks[j][...], fitted], axis=0), b[order[j]], NN)
        total += both[:rows]
        coulomb[order[j]] = both[rows:]
    for i in range(r):
        part = 2.0 * coulomb[i] - total[i * k : (i + 1) * k]
        out[i * k : (i + 1) * k, :] = part.astype(BF)


def fock_parts(place, blocks, b):
    r, _, n = b.shape
    rows = blocks[0].shape[0]
    return pl.pallas_call(
        fock_kernel,
        out_shape=array((rows, n), BF),
        in_specs=[SMEM] + [VMEM] * 9,
        out_specs=VMEM,
        scratch_shapes=[pltpu.VMEM((r, rows // r, n), F32)],
        compiler_params=PARAMS,
    )(place, *blocks, b)


def owner_kernel(arrived, s0, s1, s2, s3, out, totals):
    total = (s0[...] + s1[...]) + (s2[...] + s3[...])
    size = totals.shape[0]
    totals[...] = total[:size]
    high, low = split(total[size:])
    tail = jnp.concatenate([high, low], axis=0).astype(BF)
    fock = arrived[0].astype(F32)
    for j in range(1, arrived.shape[0]):
        fock += arrived[j].astype(F32)
    fock = fock.astype(BF)
    rows = fock.shape[0]
    for p in range(out.shape[0]):
        for i in range(4):
            out[p, i * rows : (i + 1) * rows, :] = fock[:, i * 128 : (i + 1) * 128]
        out[p, 4 * rows :, :] = tail


def owner_sums(arrived, sums, keep):
    copies, rows, _ = arrived.shape
    k = 2 * sums[0].shape[0] // 3
    return pl.pallas_call(
        owner_kernel,
        out_shape=(array((copies, 4 * rows + k, 128), BF), keep((k, 128), F32)),
        in_specs=[VMEM] * 5,
        out_specs=(VMEM, VMEM),
        compiler_params=PARAMS,
    )(arrived, *sums)


def inverse_kernel(totals, out):
    size = 2 * totals.shape[0]
    half = unlanes(totals[...], 2)
    rows = lax.broadcasted_iota(jnp.int32, (size, 2 * size), 0)
    columns = lax.broadcasted_iota(jnp.int32, (size, 2 * size), 1)
    identity = (columns == rows + size).astype(F32)
    work = jnp.concatenate([half, identity[:, size:]], axis=1)
    for j in range(0, size, 2):
        first, second = work[j : j + 1], work[j + 1 : j + 2]
        aa, ab, bb = first[:, j : j + 1], first[:, j + 1 : j + 2], second[:, j + 1 : j + 2]
        scale = 1.0 / (aa * bb - ab * ab)
        top = (bb * scale) * first - (ab * scale) * second
        bottom = (aa * scale) * second - (ab * scale) * first
        rest = work - work[:, j : j + 1] * top - work[:, j + 1 : j + 2] * bottom
        work = jnp.where(rows == j, top, jnp.where(rows == j + 1, bottom, rest))
    out[...] = work[:, size:]


def inverse_of(totals, keep):
    size = 2 * totals.shape[0]
    return pl.pallas_call(
        inverse_kernel,
        out_shape=keep((size, size), F32),
        in_specs=[VMEM],
        out_specs=VMEM,
        compiler_params=PARAMS,
    )(totals)


def solve(pieces, inverse, k, rows):
    tail = jnp.zeros((k, 4 * k), F32)
    for j in range(pieces.shape[0]):
        tail += pieces[j, 4 * rows :, :].astype(F32)
    projected = unlanes(tail[: k // 2] + tail[k // 2 :], 4)
    return dot(inverse[...], projected, NN, HIGHEST)


def fock_rows(pieces, i, k, rows):
    per_row = k // rows
    parts = [lanes(pieces[i * per_row + h, : 4 * rows, :], 4) for h in range(per_row)]
    return jnp.concatenate(parts, axis=0).astype(F32)


def step_kernel(pieces, inverse, own, other, gap, out):
    r, k, _ = own.shape
    rows = (pieces.shape[1] - k) // 4
    high, low = split(solve(pieces, inverse, k, rows))
    high, low = high.astype(BF), low.astype(BF)
    for i in range(r):
        both = jnp.concatenate([own[i], other[i]], axis=0)
        mixed = dot(high, both, TN) + dot(low, both, TN)
        value = (mixed - fock_rows(pieces, i, k, rows)) / gap[i : i + 1, :]
        out[i] = value.astype(BF)


def step_update(pieces, inverse, own, other, gap):
    return pl.pallas_call(
        step_kernel,
        out_shape=array(own.shape, BF),
        in_specs=[VMEM] * 5,
        out_specs=VMEM,
        compiler_params=PARAMS,
    )(pieces, inverse, own, other, gap)


def last_kernel(place, pieces, inverse, own, other, gap, out, coupling):
    r, k, _ = own.shape
    rows = (pieces.shape[1] - k) // 4
    solved = solve(pieces, inverse, k, rows)
    turned = solved.T
    swapped = jnp.concatenate([turned[:, k:], turned[:, :k]], axis=1)
    coupling[...] = jnp.where(place[0] == 0, turned, swapped)
    high, low = split(solved)
    high, low = high.astype(BF), low.astype(BF)
    for i in range(r):
        both = jnp.concatenate([own[i], other[i]], axis=0)
        mixed = dot(high, both, TN) + dot(low, both, TN)
        value = (mixed - fock_rows(pieces, i, k, rows)) / gap[i : i + 1, :]
        out[:, i, :] = value


def last_update(place, pieces, inverse, own, other, gap):
    r, k, n = own.shape
    vectors, coupling = pl.pallas_call(
        last_kernel,
        out_shape=(array((k, r, n), F32), array((k, 2 * k), F32)),
        in_specs=[SMEM] + [VMEM] * 5,
        out_specs=(VMEM, VMEM),
        compiler_params=PARAMS,
    )(place, pieces, inverse, own, other, gap)
    return vectors, coupling.T


def ring(step):
    pairs = []
    for h in range(4):
        for c in range(2):
            way = step if c == 1 else -step
            pairs.append((2 * h + c, 2 * ((h + way) % 4) + c))
    return pairs


AHEAD = ring(1)
BACK = ring(-1)
SIBLING = [(i, i ^ 1) for i in range(8)]
OTHER = [(0, 1), (1, 0)]


def in_hbm(value):
    return pltpu.with_memory_space_constraint(value, pltpu.HBM)


def per_device(factors, trial_vectors, energy_gap):
    place = jnp.stack([lax.axis_index(a) for a in ("gx", "gy", "gz")])
    own = jnp.transpose(trial_vectors, (1, 0, 2)).astype(BF)
    b = jnp.transpose(factors, (1, 0, 2))

    for iteration in range(ITERS):
        last = iteration == ITERS - 1
        theirs_far, mine_far = mix(place, own, b, (2,))
        theirs, *mine = mix(place, own, b, (-1, 1, 0))
        theirs_far = lax.ppermute(theirs_far, "gz", SIBLING)
        far = lax.ppermute(add(mine_far, theirs_far, 0), "gz", AHEAD)
        theirs = lax.ppermute(theirs, "gz", SIBLING)
        near = lax.ppermute(add(mine[0], theirs, 0), "gz", BACK)
        far = lax.ppermute(add(mine[1], theirs, 1, far), "gz", AHEAD)
        first = add(mine[2], theirs, 2, near, far)
        second = lax.ppermute(first, "gz", AHEAD)
        paired = lax.ppermute(first, "gz", SIBLING)
        third = lax.ppermute(first, "gz", BACK)
        fourth = lax.ppermute(second, "gz", AHEAD)
        other = lax.ppermute(own, "gx", OTHER)
        blocks = [first, second, third, fourth, paired]
        blocks += [lax.ppermute(a, "gz", SIBLING) for a in blocks[1:4]]
        fock = fock_parts(place, blocks, b)
        sums = local_sums(place, own, other, energy_gap, fock)
        arrived = lax.all_to_all(
            fock.reshape(16, -1, fock.shape[1]), "gy", 0, 0, tiled=True
        )
        sums = sums + lax.ppermute(sums, "gz", SIBLING)
        sums = [sums] + [
            lax.ppermute(sums, "gz", [(i, i ^ flip) for i in range(8)])
            for flip in (2, 4, 6)
        ]
        own, other = in_hbm(own), in_hbm(other)
        keep = array if last else pltpu.HBM
        pieces, totals = owner_sums(arrived, sums, keep)
        pieces = lax.all_to_all(pieces, "gy", 0, 0, tiled=True)
        inverse = inverse_of(totals if last else in_hbm(totals), keep)
        if last:
            return last_update(place, pieces, inverse, own, other, energy_gap)
        own = step_update(in_hbm(pieces), in_hbm(inverse), own, other, energy_gap)


def solution(mesh):
    placed = (P("gy", None, "gz"), P("gx", None, "gz"), P(None, "gz"))
    return jax.shard_map(
        per_device,
        mesh=mesh,
        in_specs=placed,
        out_specs=(P("gx", None, "gz"), P(None, "gx")),
        check_vma=False,
    )
```

profile of v0, /device:TPU:2, one launch (start us, length us, event | category | flops | bytes accessed | tf_op | source)
XLA Modules:
  0.0 193.4 jit_solution(4537926991353339862)
XLA Ops:
  0.6 1.3 copy.12
  2.0 3.0 %copy.11 = bf16[384,8,512]{2,0,1:T(8,128)(2,1)S(1)} copy(bf16[384,8,512]{2,1,0:T(8,128)(2,1)} %param.3) | data formatting | bytes 6291456 | tf_op args[0]
  5.1 1.7 shard_map.50
  6.8 0.1 collective-permute-start
  6.9 1.6 shard_map.52
  8.5 0.6 collective-permute-start.2
  9.1 1.1 collective-permute-done.2.theirs
  10.2 6.4 %collective-permute-start.3 = (bf16[256,384]{1,0:T(8,128)(2,1)S(1)}, bf16[256,384]{1,0:T(8,128)(2,1)S(1)}, u32[]{:S(2)}, u32[]{:S(2)}) collective-permute-start(bf16[256,384]{1,0:T(8,128)(2,1)S(1)} %shard_map.53), channel_id=1, source_target_pairs={{0,6},{1,3},{2,0},{3,5},{4,2},{5,7},{6,4},{7,1},{8,14},{9,11},{10,... | collective-permute-start | bytes 589832 | tf_op jit(solution)/shard_map/ppermute | solution.py:315
  16.7 9.0 %collective-permute-done.3.refs_0_ = bf16[256,384]{1,0:T(8,128)(2,1)S(1)} collective-permute-done((bf16[256,384]{1,0:T(8,128)(2,1)S(1)}, bf16[256,384]{1,0:T(8,128)(2,1)S(1)}, u32[]{:S(2)}, u32[]{:S(2)}) %collective-permute-start.3) | collective-permute-done | bytes 196640 | tf_op jit(solution)/shard_map/ppermute | solution.py:315
  25.7 4.6 %collective-permute-start.4 = (bf16[256,384]{1,0:T(8,128)(2,1)S(1)}, bf16[256,384]{1,0:T(8,128)(2,1)S(1)}, u32[]{:S(2)}, u32[]{:S(2)}) collective-permute-start(bf16[256,384]{1,0:T(8,128)(2,1)S(1)} %shard_map.54), channel_id=1, source_target_pairs={{0,6},{1,3},{2,0},{3,5},{4,2},{5,7},{6,4},{7,1},{8,14},{9,11},{10,... | collective-permute-start | bytes 589832 | tf_op jit(solution)/shard_map/ppermute | solution.py:318
  30.4 4.9 %collective-permute-done.4.refs_1_ = bf16[256,384]{1,0:T(8,128)(2,1)S(1)} collective-permute-done((bf16[256,384]{1,0:T(8,128)(2,1)S(1)}, bf16[256,384]{1,0:T(8,128)(2,1)S(1)}, u32[]{:S(2)}, u32[]{:S(2)}) %collective-permute-start.4) | collective-permute-done | bytes 196640 | tf_op jit(solution)/shard_map/ppermute | solution.py:318
  35.3 0.1 shard_map.55.refs_0_
  35.4 4.7 %collective-permute-start.5 = (bf16[256,384]{1,0:T(8,128)(2,1)S(1)}, bf16[256,384]{1,0:T(8,128)(2,1)S(1)}, u32[]{:S(2)}, u32[]{:S(2)}) collective-permute-start(bf16[256,384]{1,0:T(8,128)(2,1)S(1)} %shard_map.55.refs_0_), channel_id=1, source_target_pairs={{0,6},{1,3},{2,0},{3,5},{4,2},{5,7},{6,4},{7,1},{8,14},{9,11},{10,... | collective-permute-start | bytes 589832 | tf_op jit(solution)/shard_map/ppermute | solution.py:320
  40.1 5.1 %collective-permute-done.5.refs_1_ = bf16[256,384]{1,0:T(8,128)(2,1)S(1)} collective-permute-done((bf16[256,384]{1,0:T(8,128)(2,1)S(1)}, bf16[256,384]{1,0:T(8,128)(2,1)S(1)}, u32[]{:S(2)}, u32[]{:S(2)}) %collective-permute-start.5) | collective-permute-done | bytes 196640 | tf_op jit(solution)/shard_map/ppermute | solution.py:320
  45.2 2.7 %collective-permute-start.7 = (bf16[256,384]{1,0:T(8,128)(2,1)S(1)}, bf16[256,384]{1,0:T(8,128)(2,1)S(1)}, u32[]{:S(2)}, u32[]{:S(2)}) collective-permute-start(bf16[256,384]{1,0:T(8,128)(2,1)S(1)} %collective-permute-done.5.refs_1_), channel_id=1, source_target_pairs={{0,6},{1,3},{2,0},{3,5},{4,2},{5,7},{6,4},{7,1},{8,14},{9,11},{10,... | collective-permute-start | bytes 589832 | tf_op jit(solution)/shard_map/ppermute | solution.py:323
  47.9 0.5 collective-permute-start.9
  48.4 2.5 %collective-permute-done.6.refs_2_ = bf16[256,384]{1,0:T(8,128)(2,1)S(1)} collective-permute-done((bf16[256,384]{1,0:T(8,128)(2,1)S(1)}, bf16[256,384]{1,0:T(8,128)(2,1)S(1)}, u32[]{:S(2)}, u32[]{:S(2)}) %collective-permute-start.6) | collective-permute-done | bytes 196640 | tf_op jit(solution)/shard_map/ppermute | solution.py:322
  51.0 2.8 %collective-permute-done.7.refs_3_ = bf16[256,384]{1,0:T(8,128)(2,1)S(1)} collective-permute-done((bf16[256,384]{1,0:T(8,128)(2,1)S(1)}, bf16[256,384]{1,0:T(8,128)(2,1)S(1)}, u32[]{:S(2)}, u32[]{:S(2)}) %collective-permute-start.7) | collective-permute-done | bytes 196640 | tf_op jit(solution)/shard_map/ppermute | solution.py:323
  53.8 1.6 collective-permute-start.12
  55.5 2.0 %shard_map.56.fock = bf16[256,512]{1,0:T(8,128)(2,1)S(1)} custom-call(s32[3]{0:T(128)S(1)} %pad_add_fusion.refs_0_.place, bf16[256,384]{1,0:T(8,128)(2,1)S(1)} %shard_map.55.refs_0_, bf16[256,384]{1,0:T(8,128)(2,1)S(1)} %collective-permute-done.5.refs_1_, bf16[256,384]{1,0:T(8,128)(2,1)S(1)} %collective-permute-done.6.refs_2_, ...), custom_call_target="tpu_custom_call" | custom-call | tf_op jit(solution)/shard_map/pallas_call | solution.py:154
  57.5 0.7 copy-done.4
  58.2 7.5 %all-to-all-start = ((bf16[16,16,512]{2,1,0:T(8,128)(2,1)}), bf16[16,16,512]{2,1,0:T(8,128)(2,1)}, u32[]{:S(2)}, u32[]{:S(2)}) async-start(bf16[16,16,512]{2,1,0:T(8,128)(2,1)} %bitcast.24), calls=%async_computation | async-start | bytes 524288 | tf_op jit(solution)/shard_map/all_to_all | solution.py:329
  65.7 1.0 copy-done.5
  66.7 1.7 shard_map.57
  68.5 1.2 collective-permute-done.13
  69.7 1.3 collective-permute-start.14
  71.0 5.7 %collective-permute-start.15 = (f32[48,128]{1,0:T(8,128)S(1)}, f32[48,128]{1,0:T(8,128)S(1)}, u32[]{:S(2)}, u32[]{:S(2)}) collective-permute-start(f32[48,128]{1,0:T(8,128)S(1)} %add.6.s0), channel_id=1, source_target_pairs={{0,4},{1,5},{2,6},{3,7},{4,0},{5,1},{6,2},{7,3},{8,12},{9,13},{10,... | collective-permute-start | bytes 73736 | tf_op jit(solution)/shard_map/ppermute | solution.py:334
  76.6 2.1 %collective-permute-done.15.s2 = f32[48,128]{1,0:T(8,128)S(1)} collective-permute-done((f32[48,128]{1,0:T(8,128)S(1)}, f32[48,128]{1,0:T(8,128)S(1)}, u32[]{:S(2)}, u32[]{:S(2)}) %collective-permute-start.15) | collective-permute-done | bytes 24608 | tf_op jit(solution)/shard_map/ppermute | solution.py:334
  78.7 3.9 %collective-permute-done.16.s3 = f32[48,128]{1,0:T(8,128)S(1)} collective-permute-done((f32[48,128]{1,0:T(8,128)S(1)}, f32[48,128]{1,0:T(8,128)S(1)}, u32[]{:S(2)}, u32[]{:S(2)}) %collective-permute-start.16) | collective-permute-done | bytes 24608 | tf_op jit(solution)/shard_map/ppermute | solution.py:334
  82.6 1.8 shard_map.58
  84.3 7.2 %all-to-all-start.1 = ((bf16[16,96,128]{2,1,0:T(8,128)(2,1)}), bf16[16,96,128]{2,1,0:T(8,128)(2,1)}, u32[]{:S(2)}, u32[]{:S(2)}) async-start(bf16[16,96,128]{2,1,0:T(8,128)(2,1)} %get-tuple-element.26), calls=%async_computation.1 | async-start | bytes 786432 | tf_op jit(solution)/shard_map/all_to_all | solution.py:340
  91.5 8.8 %shard_map.59.inverse = f32[64,64]{1,0:T(8,128)} custom-call(f32[32,128]{1,0:T(8,128)} %get-tuple-element.27.totals), custom_call_target="tpu_custom_call" | custom-call | tf_op jit(solution)/shard_map/pallas_call | solution.py:213
  100.3 1.8 shard_map.60.refs_1_.own
  102.1 1.7 shard_map.61
  103.8 0.1 collective-permute-start.17
  103.9 1.6 shard_map.63
  105.5 0.6 collective-permute-start.19
  106.1 1.1 collective-permute-done.19.theirs
  107.2 0.6 collective-permute-start.20
  107.9 2.5 %collective-permute-start.18 = (bf16[256,384]{1,0:T(8,128)(2,1)S(1)}, bf16[256,384]{1,0:T(8,128)(2,1)S(1)}, u32[]{:S(2)}, u32[]{:S(2)}) collective-permute-start(bf16[256,384]{1,0:T(8,128)(2,1)S(1)} %shard_map.62), channel_id=1, source_target_pairs={{0,2},{1,7},{2,4},{3,1},{4,6},{5,3},{6,0},{7,5},{8,10},{9,15},{10,... | collective-permute-start | bytes 589832 | tf_op jit(solution)/shard_map/ppermute | solution.py:317
  110.3 9.2 %collective-permute-done.20.refs_0_ = bf16[256,384]{1,0:T(8,128)(2,1)S(1)} collective-permute-done((bf16[256,384]{1,0:T(8,128)(2,1)S(1)}, bf16[256,384]{1,0:T(8,128)(2,1)S(1)}, u32[]{:S(2)}, u32[]{:S(2)}) %collective-permute-start.20) | collective-permute-done | bytes 196640 | tf_op jit(solution)/shard_map/ppermute | solution.py:315
  119.7 1.0 collective-permute-done.18.refs_0_
  120.7 8.6 %collective-permute-done.21.refs_1_ = bf16[256,384]{1,0:T(8,128)(2,1)S(1)} collective-permute-done((bf16[256,384]{1,0:T(8,128)(2,1)S(1)}, bf16[256,384]{1,0:T(8,128)(2,1)S(1)}, u32[]{:S(2)}, u32[]{:S(2)}) %collective-permute-start.21) | collective-permute-done | bytes 196640 | tf_op jit(solution)/shard_map/ppermute | solution.py:318
  129.3 0.1 shard_map.66.refs_0_
  129.4 0.4 collective-permute-start.22
  129.8 2.6 %collective-permute-start.23 = (bf16[256,384]{1,0:T(8,128)(2,1)S(1)}, bf16[256,384]{1,0:T(8,128)(2,1)S(1)}, u32[]{:S(2)}, u32[]{:S(2)}) collective-permute-start(bf16[256,384]{1,0:T(8,128)(2,1)S(1)} %shard_map.66.refs_0_), channel_id=1, source_target_pairs={{0,2},{1,7},{2,4},{3,1},{4,6},{5,3},{6,0},{7,5},{8,10},{9,15},{10,... | collective-permute-start | bytes 589832 | tf_op jit(solution)/shard_map/ppermute | solution.py:322
  132.4 6.2 %collective-permute-done.22.refs_1_ = bf16[256,384]{1,0:T(8,128)(2,1)S(1)} collective-permute-done((bf16[256,384]{1,0:T(8,128)(2,1)S(1)}, bf16[256,384]{1,0:T(8,128)(2,1)S(1)}, u32[]{:S(2)}, u32[]{:S(2)}) %collective-permute-start.22) | collective-permute-done | bytes 196640 | tf_op jit(solution)/shard_map/ppermute | solution.py:320
  138.6 2.3 %collective-permute-start.24 = (bf16[256,384]{1,0:T(8,128)(2,1)S(1)}, bf16[256,384]{1,0:T(8,128)(2,1)S(1)}, u32[]{:S(2)}, u32[]{:S(2)}) collective-permute-start(bf16[256,384]{1,0:T(8,128)(2,1)S(1)} %collective-permute-done.22.refs_1_), channel_id=1, source_target_pairs={{0,6},{1,3},{2,0},{3,5},{4,2},{5,7},{6,4},{7,1},{8,14},{9,11},{10,... | collective-permute-start | bytes 589832 | tf_op jit(solution)/shard_map/ppermute | solution.py:323
  140.8 0.5 collective-permute-start.26
  141.4 5.4 %collective-permute-done.24.refs_3_ = bf16[256,384]{1,0:T(8,128)(2,1)S(1)} collective-permute-done((bf16[256,384]{1,0:T(8,128)(2,1)S(1)}, bf16[256,384]{1,0:T(8,128)(2,1)S(1)}, u32[]{:S(2)}, u32[]{:S(2)}) %collective-permute-start.24) | collective-permute-done | bytes 196640 | tf_op jit(solution)/shard_map/ppermute | solution.py:323
  146.8 1.4 collective-permute-done.28.refs_7_
  148.2 2.0 %shard_map.67.fock = bf16[256,512]{1,0:T(8,128)(2,1)S(1)} custom-call(s32[3]{0:T(128)S(1)} %pad_add_fusion.refs_0_.place, bf16[256,384]{1,0:T(8,128)(2,1)S(1)} %shard_map.66.refs_0_, bf16[256,384]{1,0:T(8,128)(2,1)S(1)} %collective-permute-done.22.refs_1_, bf16[256,384]{1,0:T(8,128)(2,1)S(1)} %collective-permute-done.23.refs_2_, ...), custom_call_target="tpu_custom_call" | custom-call | tf_op jit(solution)/shard_map/pallas_call | solution.py:154
  150.3 0.7 copy-done.2
  151.0 7.2 %all-to-all-start.2 = ((bf16[16,16,512]{2,1,0:T(8,128)(2,1)}), bf16[16,16,512]{2,1,0:T(8,128)(2,1)S(1)}, u32[]{:S(2)}, u32[]{:S(2)}) async-start(bf16[16,16,512]{2,1,0:T(8,128)(2,1)} %bitcast.23), calls=%async_computation.2 | async-start | bytes 524288 | tf_op jit(solution)/shard_map/all_to_all | solution.py:329
  158.2 1.0 copy-done.3
  159.2 1.7 shard_map.68
  161.0 1.2 collective-permute-done.30
  162.1 5.5 %collective-permute-start.31 = (f32[48,128]{1,0:T(8,128)S(1)}, f32[48,128]{1,0:T(8,128)S(1)}, u32[]{:S(2)}, u32[]{:S(2)}) collective-permute-start(f32[48,128]{1,0:T(8,128)S(1)} %add.7.s0), channel_id=1, source_target_pairs={{0,2},{1,3},{2,0},{3,1},{4,6},{5,7},{6,4},{7,5},{8,10},{9,11},{10,... | collective-permute-start | bytes 73736 | tf_op jit(solution)/shard_map/ppermute | solution.py:334
  167.7 3.7 %collective-permute-start.33 = (f32[48,128]{1,0:T(8,128)S(1)}, f32[48,128]{1,0:T(8,128)S(1)}, u32[]{:S(2)}, u32[]{:S(2)}) collective-permute-start(f32[48,128]{1,0:T(8,128)S(1)} %add.7.s0), channel_id=1, source_target_pairs={{0,6},{1,7},{2,4},{3,5},{4,2},{5,3},{6,0},{7,1},{8,14},{9,15},{10,... | collective-permute-start | bytes 73736 | tf_op jit(solution)/shard_map/ppermute | solution.py:334
  171.3 4.1 %collective-permute-done.32.s2 = f32[48,128]{1,0:T(8,128)S(1)} collective-permute-done((f32[48,128]{1,0:T(8,128)S(1)}, f32[48,128]{1,0:T(8,128)S(1)}, u32[]{:S(2)}, u32[]{:S(2)}) %collective-permute-start.32) | collective-permute-done | bytes 24608 | tf_op jit(solution)/shard_map/ppermute | solution.py:334
  175.4 0.8 shard_map.69
  176.2 7.2 %all-to-all-start.3 = ((bf16[16,96,128]{2,1,0:T(8,128)(2,1)}), bf16[16,96,128]{2,1,0:T(8,128)(2,1)S(1)}, u32[]{:S(2)}, u32[]{:S(2)}) async-start(bf16[16,96,128]{2,1,0:T(8,128)(2,1)} %get-tuple-element.34), calls=%async_computation.3 | async-start | bytes 786432 | tf_op jit(solution)/shard_map/all_to_all | solution.py:340
  183.4 7.4 %shard_map.70.inverse = f32[64,64]{1,0:T(8,128)S(1)} custom-call(f32[32,128]{1,0:T(8,128)S(1)} %get-tuple-element.35.totals), custom_call_target="tpu_custom_call" | custom-call | tf_op jit(solution)/shard_map/pallas_call | solution.py:213
  190.9 2.5 %shard_map.71 = (f32[32,8,512]{2,1,0:T(8,128)}, f32[32,64]{1,0:T(8,128)}) custom-call(s32[3]{0:T(128)S(1)} %pad_add_fusion.refs_0_.place, bf16[16,96,128]{2,1,0:T(8,128)(2,1)S(1)} %all-to-all-done.3.pieces, f32[64,64]{1,0:T(8,128)S(1)} %shard_map.70.inverse, bf16[8,32,512]{2,1,0:T(8,128)(2,1)} %copy-done, bf16[8,32,512]{2,1,0:T(8,128)(2,1)} %collective-permute-done.29.other, ...), custom_call_target="tpu_custom_call" | custom-call | tf_op jit(solution)/shard_map/pallas_call | solution.py:276
  (53 shorter events, 0.8 us)
Async XLA Ops:
  2.0 63.7 %copy-start.1 = (bf16[32,8,512]{2,0,1:T(8,128)(2,1)}, bf16[32,8,512]{2,0,1:T(8,128)(2,1)S(1)}, u32[]{:S(2)}) copy-start(bf16[32,8,512]{2,0,1:T(8,128)(2,1)S(1)} %copy.12) | copy-start | bytes 786436
  6.8 9.8 %collective-permute-start = (bf16[3,256,384]{2,1,0:T(8,128)(2,1)S(1)}, bf16[3,256,384]{2,1,0:T(8,128)(2,1)S(1)}, u32[]{:S(2)}, u32[]{:S(2)}) collective-permute-start(bf16[3,256,384]{2,1,0:T(8,128)(2,1)S(1)} %get-tuple-element.21), channel_id=1, source_target_pairs={{0,1},{1,0},{2,3},{3,2},{4,5},{5,4},{6,7},{7,6},{8,9},{9,8},{10,11... | collective-permute-start | bytes 1769480 | tf_op jit(solution)/shard_map/ppermute | solution.py:316
  8.5 1.7 collective-permute-start.2
  10.2 15.5 %collective-permute-start.3 = (bf16[256,384]{1,0:T(8,128)(2,1)S(1)}, bf16[256,384]{1,0:T(8,128)(2,1)S(1)}, u32[]{:S(2)}, u32[]{:S(2)}) collective-permute-start(bf16[256,384]{1,0:T(8,128)(2,1)S(1)} %shard_map.53), channel_id=1, source_target_pairs={{0,6},{1,3},{2,0},{3,5},{4,2},{5,7},{6,4},{7,1},{8,14},{9,11},{10,... | collective-permute-start | bytes 589832 | tf_op jit(solution)/shard_map/ppermute | solution.py:315
  16.6 13.8 %collective-permute-start.1 = (bf16[256,384]{1,0:T(8,128)(2,1)S(1)}, bf16[256,384]{1,0:T(8,128)(2,1)S(1)}, u32[]{:S(2)}, u32[]{:S(2)}) collective-permute-start(bf16[256,384]{1,0:T(8,128)(2,1)S(1)} %shard_map.51), channel_id=1, source_target_pairs={{0,2},{1,7},{2,4},{3,1},{4,6},{5,3},{6,0},{7,5},{8,10},{9,15},{10,... | collective-permute-start | bytes 589832 | tf_op jit(solution)/shard_map/ppermute | solution.py:317
  25.7 9.6 %collective-permute-start.4 = (bf16[256,384]{1,0:T(8,128)(2,1)S(1)}, bf16[256,384]{1,0:T(8,128)(2,1)S(1)}, u32[]{:S(2)}, u32[]{:S(2)}) collective-permute-start(bf16[256,384]{1,0:T(8,128)(2,1)S(1)} %shard_map.54), channel_id=1, source_target_pairs={{0,6},{1,3},{2,0},{3,5},{4,2},{5,7},{6,4},{7,1},{8,14},{9,11},{10,... | collective-permute-start | bytes 589832 | tf_op jit(solution)/shard_map/ppermute | solution.py:318
  35.4 30.3 %copy-start.6 = (f32[8,512]{1,0:T(8,128)S(1)}, f32[8,512]{1,0:T(8,128)}, u32[]{:S(2)}) copy-start(f32[8,512]{1,0:T(8,128)} %gap.7) | copy-start | bytes 49156
  35.4 9.8 %collective-permute-start.5 = (bf16[256,384]{1,0:T(8,128)(2,1)S(1)}, bf16[256,384]{1,0:T(8,128)(2,1)S(1)}, u32[]{:S(2)}, u32[]{:S(2)}) collective-permute-start(bf16[256,384]{1,0:T(8,128)(2,1)S(1)} %shard_map.55.refs_0_), channel_id=1, source_target_pairs={{0,6},{1,3},{2,0},{3,5},{4,2},{5,7},{6,4},{7,1},{8,14},{9,11},{10,... | collective-permute-start | bytes 589832 | tf_op jit(solution)/shard_map/ppermute | solution.py:320
  40.1 10.8 %collective-permute-start.6 = (bf16[256,384]{1,0:T(8,128)(2,1)S(1)}, bf16[256,384]{1,0:T(8,128)(2,1)S(1)}, u32[]{:S(2)}, u32[]{:S(2)}) collective-permute-start(bf16[256,384]{1,0:T(8,128)(2,1)S(1)} %shard_map.55.refs_0_), channel_id=1, source_target_pairs={{0,2},{1,7},{2,4},{3,1},{4,6},{5,3},{6,0},{7,5},{8,10},{9,15},{10,... | collective-permute-start | bytes 589832 | tf_op jit(solution)/shard_map/ppermute | solution.py:322
  45.2 8.6 %collective-permute-start.7 = (bf16[256,384]{1,0:T(8,128)(2,1)S(1)}, bf16[256,384]{1,0:T(8,128)(2,1)S(1)}, u32[]{:S(2)}, u32[]{:S(2)}) collective-permute-start(bf16[256,384]{1,0:T(8,128)(2,1)S(1)} %collective-permute-done.5.refs_1_), channel_id=1, source_target_pairs={{0,6},{1,3},{2,0},{3,5},{4,2},{5,7},{6,4},{7,1},{8,14},{9,11},{10,... | collective-permute-start | bytes 589832 | tf_op jit(solution)/shard_map/ppermute | solution.py:323
  47.9 7.5 %collective-permute-start.8 = (bf16[256,384]{1,0:T(8,128)(2,1)S(1)}, bf16[256,384]{1,0:T(8,128)(2,1)S(1)}, u32[]{:S(2)}, u32[]{:S(2)}) collective-permute-start(bf16[256,384]{1,0:T(8,128)(2,1)S(1)} %shard_map.55.refs_0_), channel_id=1, source_target_pairs={{0,1},{1,0},{2,3},{3,2},{4,5},{5,4},{6,7},{7,6},{8,9},{9,8},{10,11... | collective-permute-start | bytes 589832 | tf_op jit(solution)/shard_map/ppermute | solution.py:321
  47.9 7.5 %collective-permute-start.9 = (bf16[256,384]{1,0:T(8,128)(2,1)S(1)}, bf16[256,384]{1,0:T(8,128)(2,1)S(1)}, u32[]{:S(2)}, u32[]{:S(2)}) collective-permute-start(bf16[256,384]{1,0:T(8,128)(2,1)S(1)} %collective-permute-done.5.refs_1_), channel_id=1, source_target_pairs={{0,1},{1,0},{2,3},{3,2},{4,5},{5,4},{6,7},{7,6},{8,9},{9,8},{10,11... | collective-permute-start | bytes 589832 | tf_op jit(solution)/shard_map/ppermute | solution.py:326
  51.0 4.5 %collective-permute-start.10 = (bf16[256,384]{1,0:T(8,128)(2,1)S(1)}, bf16[256,384]{1,0:T(8,128)(2,1)S(1)}, u32[]{:S(2)}, u32[]{:S(2)}) collective-permute-start(bf16[256,384]{1,0:T(8,128)(2,1)S(1)} %collective-permute-done.6.refs_2_), channel_id=1, source_target_pairs={{0,1},{1,0},{2,3},{3,2},{4,5},{5,4},{6,7},{7,6},{8,9},{9,8},{10,11... | collective-permute-start | bytes 589832 | tf_op jit(solution)/shard_map/ppermute | solution.py:326
  53.8 1.7 collective-permute-start.11
  53.8 11.9 %collective-permute-start.12 = (bf16[8,32,512]{2,1,0:T(8,128)(2,1)S(1)}, bf16[8,32,512]{2,1,0:T(8,128)(2,1)}, u32[]{:S(2)}, u32[]{:S(2)}) collective-permute-start(bf16[8,32,512]{2,1,0:T(8,128)(2,1)S(1)} %bitcast.20), channel_id=1, source_target_pairs={{0,128},{128,0},{1,129},{129,1},{2,130},{130,2},{3,131},{131,3},{4... | collective-permute-start | bytes 786440 | tf_op jit(solution)/shard_map/ppermute | solution.py:324
  57.5 0.7 copy-start.4
  58.2 24.4 %all-to-all-start = ((bf16[16,16,512]{2,1,0:T(8,128)(2,1)}), bf16[16,16,512]{2,1,0:T(8,128)(2,1)}, u32[]{:S(2)}, u32[]{:S(2)}) async-start(bf16[16,16,512]{2,1,0:T(8,128)(2,1)} %bitcast.24), calls=%async_computation | async-start | bytes 524288 | tf_op jit(solution)/shard_map/all_to_all | solution.py:329
  65.7 1.0 copy-start.5
  68.4 1.3 collective-permute-start.13
  69.7 7.0 %collective-permute-start.14 = (f32[48,128]{1,0:T(8,128)S(1)}, f32[48,128]{1,0:T(8,128)S(1)}, u32[]{:S(2)}, u32[]{:S(2)}) collective-permute-start(f32[48,128]{1,0:T(8,128)S(1)} %add.6.s0), channel_id=1, source_target_pairs={{0,2},{1,3},{2,0},{3,1},{4,6},{5,7},{6,4},{7,5},{8,10},{9,11},{10,... | collective-permute-start | bytes 73736 | tf_op jit(solution)/shard_map/ppermute | solution.py:334
  71.0 7.7 %collective-permute-start.15 = (f32[48,128]{1,0:T(8,128)S(1)}, f32[48,128]{1,0:T(8,128)S(1)}, u32[]{:S(2)}, u32[]{:S(2)}) collective-permute-start(f32[48,128]{1,0:T(8,128)S(1)} %add.6.s0), channel_id=1, source_target_pairs={{0,4},{1,5},{2,6},{3,7},{4,0},{5,1},{6,2},{7,3},{8,12},{9,13},{10,... | collective-permute-start | bytes 73736 | tf_op jit(solution)/shard_map/ppermute | solution.py:334
  76.6 5.9 %collective-permute-start.16 = (f32[48,128]{1,0:T(8,128)S(1)}, f32[48,128]{1,0:T(8,128)S(1)}, u32[]{:S(2)}, u32[]{:S(2)}) collective-permute-start(f32[48,128]{1,0:T(8,128)S(1)} %add.6.s0), channel_id=1, source_target_pairs={{0,6},{1,7},{2,4},{3,5},{4,2},{5,3},{6,0},{7,1},{8,14},{9,15},{10,... | collective-permute-start | bytes 73736 | tf_op jit(solution)/shard_map/ppermute | solution.py:334
  84.3 16.0 %all-to-all-start.1 = ((bf16[16,96,128]{2,1,0:T(8,128)(2,1)}), bf16[16,96,128]{2,1,0:T(8,128)(2,1)}, u32[]{:S(2)}, u32[]{:S(2)}) async-start(bf16[16,96,128]{2,1,0:T(8,128)(2,1)} %get-tuple-element.26), calls=%async_computation.1 | async-start | bytes 786432 | tf_op jit(solution)/shard_map/all_to_all | solution.py:340
  102.1 56.1 %copy-start = (bf16[8,32,512]{2,1,0:T(8,128)(2,1)}, bf16[8,32,512]{2,1,0:T(8,128)(2,1)S(1)}, u32[]{:S(2)}) copy-start(bf16[8,32,512]{2,1,0:T(8,128)(2,1)S(1)} %shard_map.60.refs_1_.own) | copy-start | bytes 786436
  103.8 4.0 %collective-permute-start.17 = (bf16[3,256,384]{2,1,0:T(8,128)(2,1)S(1)}, bf16[3,256,384]{2,1,0:T(8,128)(2,1)S(1)}, u32[]{:S(2)}, u32[]{:S(2)}) collective-permute-start(bf16[3,256,384]{2,1,0:T(8,128)(2,1)S(1)} %get-tuple-element.29), channel_id=1, source_target_pairs={{0,1},{1,0},{2,3},{3,2},{4,5},{5,4},{6,7},{7,6},{8,9},{9,8},{10,11... | collective-permute-start | bytes 1769480 | tf_op jit(solution)/shard_map/ppermute | solution.py:316
  105.5 1.7 collective-permute-start.19
  107.2 12.3 %collective-permute-start.20 = (bf16[256,384]{1,0:T(8,128)(2,1)S(1)}, bf16[256,384]{1,0:T(8,128)(2,1)S(1)}, u32[]{:S(2)}, u32[]{:S(2)}) collective-permute-start(bf16[256,384]{1,0:T(8,128)(2,1)S(1)} %shard_map.64), channel_id=1, source_target_pairs={{0,6},{1,3},{2,0},{3,5},{4,2},{5,7},{6,4},{7,1},{8,14},{9,11},{10,... | collective-permute-start | bytes 589832 | tf_op jit(solution)/shard_map/ppermute | solution.py:315
  107.9 12.8 %collective-permute-start.18 = (bf16[256,384]{1,0:T(8,128)(2,1)S(1)}, bf16[256,384]{1,0:T(8,128)(2,1)S(1)}, u32[]{:S(2)}, u32[]{:S(2)}) collective-permute-start(bf16[256,384]{1,0:T(8,128)(2,1)S(1)} %shard_map.62), channel_id=1, source_target_pairs={{0,2},{1,7},{2,4},{3,1},{4,6},{5,3},{6,0},{7,5},{8,10},{9,15},{10,... | collective-permute-start | bytes 589832 | tf_op jit(solution)/shard_map/ppermute | solution.py:317
  119.6 9.6 %collective-permute-start.21 = (bf16[256,384]{1,0:T(8,128)(2,1)S(1)}, bf16[256,384]{1,0:T(8,128)(2,1)S(1)}, u32[]{:S(2)}, u32[]{:S(2)}) collective-permute-start(bf16[256,384]{1,0:T(8,128)(2,1)S(1)} %shard_map.65), channel_id=1, source_target_pairs={{0,6},{1,3},{2,0},{3,5},{4,2},{5,7},{6,4},{7,1},{8,14},{9,11},{10,... | collective-permute-start | bytes 589832 | tf_op jit(solution)/shard_map/ppermute | solution.py:318
  129.4 9.2 %collective-permute-start.22 = (bf16[256,384]{1,0:T(8,128)(2,1)S(1)}, bf16[256,384]{1,0:T(8,128)(2,1)S(1)}, u32[]{:S(2)}, u32[]{:S(2)}) collective-permute-start(bf16[256,384]{1,0:T(8,128)(2,1)S(1)} %shard_map.66.refs_0_), channel_id=1, source_target_pairs={{0,6},{1,3},{2,0},{3,5},{4,2},{5,7},{6,4},{7,1},{8,14},{9,11},{10,... | collective-permute-start | bytes 589832 | tf_op jit(solution)/shard_map/ppermute | solution.py:320
  129.8 11.6 %collective-permute-start.23 = (bf16[256,384]{1,0:T(8,128)(2,1)S(1)}, bf16[256,384]{1,0:T(8,128)(2,1)S(1)}, u32[]{:S(2)}, u32[]{:S(2)}) collective-permute-start(bf16[256,384]{1,0:T(8,128)(2,1)S(1)} %shard_map.66.refs_0_), channel_id=1, source_target_pairs={{0,2},{1,7},{2,4},{3,1},{4,6},{5,3},{6,0},{7,5},{8,10},{9,15},{10,... | collective-permute-start | bytes 589832 | tf_op jit(solution)/shard_map/ppermute | solution.py:322
  138.6 8.3 %collective-permute-start.24 = (bf16[256,384]{1,0:T(8,128)(2,1)S(1)}, bf16[256,384]{1,0:T(8,128)(2,1)S(1)}, u32[]{:S(2)}, u32[]{:S(2)}) collective-permute-start(bf16[256,384]{1,0:T(8,128)(2,1)S(1)} %collective-permute-done.22.refs_1_), channel_id=1, source_target_pairs={{0,6},{1,3},{2,0},{3,5},{4,2},{5,7},{6,4},{7,1},{8,14},{9,11},{10,... | collective-permute-start | bytes 589832 | tf_op jit(solution)/shard_map/ppermute | solution.py:323
  140.8 6.0 %collective-permute-start.25 = (bf16[256,384]{1,0:T(8,128)(2,1)S(1)}, bf16[256,384]{1,0:T(8,128)(2,1)S(1)}, u32[]{:S(2)}, u32[]{:S(2)}) collective-permute-start(bf16[256,384]{1,0:T(8,128)(2,1)S(1)} %shard_map.66.refs_0_), channel_id=1, source_target_pairs={{0,1},{1,0},{2,3},{3,2},{4,5},{5,4},{6,7},{7,6},{8,9},{9,8},{10,11... | collective-permute-start | bytes 589832 | tf_op jit(solution)/shard_map/ppermute | solution.py:321
  140.8 6.0 %collective-permute-start.26 = (bf16[256,384]{1,0:T(8,128)(2,1)S(1)}, bf16[256,384]{1,0:T(8,128)(2,1)S(1)}, u32[]{:S(2)}, u32[]{:S(2)}) collective-permute-start(bf16[256,384]{1,0:T(8,128)(2,1)S(1)} %collective-permute-done.22.refs_1_), channel_id=1, source_target_pairs={{0,1},{1,0},{2,3},{3,2},{4,5},{5,4},{6,7},{7,6},{8,9},{9,8},{10,11... | collective-permute-start | bytes 589832 | tf_op jit(solution)/shard_map/ppermute | solution.py:326
  141.4 5.5 %collective-permute-start.27 = (bf16[256,384]{1,0:T(8,128)(2,1)S(1)}, bf16[256,384]{1,0:T(8,128)(2,1)S(1)}, u32[]{:S(2)}, u32[]{:S(2)}) collective-permute-start(bf16[256,384]{1,0:T(8,128)(2,1)S(1)} %collective-permute-done.23.refs_2_), channel_id=1, source_target_pairs={{0,1},{1,0},{2,3},{3,2},{4,5},{5,4},{6,7},{7,6},{8,9},{9,8},{10,11... | collective-permute-start | bytes 589832 | tf_op jit(solution)/shard_map/ppermute | solution.py:326
  146.8 1.4 collective-permute-start.28
  146.8 11.4 %collective-permute-start.29 = (bf16[8,32,512]{2,1,0:T(8,128)(2,1)S(1)}, bf16[8,32,512]{2,1,0:T(8,128)(2,1)}, u32[]{:S(2)}, u32[]{:S(2)}) collective-permute-start(bf16[8,32,512]{2,1,0:T(8,128)(2,1)S(1)} %shard_map.60.refs_1_.own), channel_id=1, source_target_pairs={{0,128},{128,0},{1,129},{129,1},{2,130},{130,2},{3,131},{131,3},{4... | collective-permute-start | bytes 786440 | tf_op jit(solution)/shard_map/ppermute | solution.py:324
  150.3 0.7 copy-start.2
  151.0 24.4 %all-to-all-start.2 = ((bf16[16,16,512]{2,1,0:T(8,128)(2,1)}), bf16[16,16,512]{2,1,0:T(8,128)(2,1)S(1)}, u32[]{:S(2)}, u32[]{:S(2)}) async-start(bf16[16,16,512]{2,1,0:T(8,128)(2,1)} %bitcast.23), calls=%async_computation.2 | async-start | bytes 524288 | tf_op jit(solution)/shard_map/all_to_all | solution.py:329
  158.2 1.0 copy-start.3
  160.9 1.3 collective-permute-start.30
  162.1 9.2 %collective-permute-start.31 = (f32[48,128]{1,0:T(8,128)S(1)}, f32[48,128]{1,0:T(8,128)S(1)}, u32[]{:S(2)}, u32[]{:S(2)}) collective-permute-start(f32[48,128]{1,0:T(8,128)S(1)} %add.7.s0), channel_id=1, source_target_pairs={{0,2},{1,3},{2,0},{3,1},{4,6},{5,7},{6,4},{7,5},{8,10},{9,11},{10,... | collective-permute-start | bytes 73736 | tf_op jit(solution)/shard_map/ppermute | solution.py:334
  167.7 7.7 %collective-permute-start.32 = (f32[48,128]{1,0:T(8,128)S(1)}, f32[48,128]{1,0:T(8,128)S(1)}, u32[]{:S(2)}, u32[]{:S(2)}) collective-permute-start(f32[48,128]{1,0:T(8,128)S(1)} %add.7.s0), channel_id=1, source_target_pairs={{0,4},{1,5},{2,6},{3,7},{4,0},{5,1},{6,2},{7,3},{8,12},{9,13},{10,... | collective-permute-start | bytes 73736 | tf_op jit(solution)/shard_map/ppermute | solution.py:334
  167.7 7.7 %collective-permute-start.33 = (f32[48,128]{1,0:T(8,128)S(1)}, f32[48,128]{1,0:T(8,128)S(1)}, u32[]{:S(2)}, u32[]{:S(2)}) collective-permute-start(f32[48,128]{1,0:T(8,128)S(1)} %add.7.s0), channel_id=1, source_target_pairs={{0,6},{1,7},{2,4},{3,5},{4,2},{5,3},{6,0},{7,1},{8,14},{9,15},{10,... | collective-permute-start | bytes 73736 | tf_op jit(solution)/shard_map/ppermute | solution.py:334
  176.2 14.7 %all-to-all-start.3 = ((bf16[16,96,128]{2,1,0:T(8,128)(2,1)}), bf16[16,96,128]{2,1,0:T(8,128)(2,1)S(1)}, u32[]{:S(2)}, u32[]{:S(2)}) async-start(bf16[16,96,128]{2,1,0:T(8,128)(2,1)} %get-tuple-element.34), calls=%async_computation.3 | async-start | bytes 786432 | tf_op jit(solution)/shard_map/all_to_all | solution.py:340
where the time goes:
time: 194 us; the launch traced here: 193 us
  starting transfers between devices  76.5 us (39%)
  waiting for transfers between devices  70.7 us (36%)
  Pallas kernels  37.5 us (19%)
  local copies, waits for them, and re-layouts  7.71 us (4%)
    ppermute x2, waiting for transfers between devices, per_device(): far = lax.ppermute(add(mine_far, theirs_far, 0), 'gz', AHEAD)  18.2 us
    pallas_call x2, Pallas kernels, inverse_of(): pl.pallas_call(inverse_kernel, out_shape=keep((size, size), F32), in_spec...  16.2 us
    ppermute x6, starting transfers between devices, per_device(): lax.ppermute(sums, 'gz', [(i, i ^ flip) for i in range(8)])  16.1 us
    all_to_all x2, starting transfers between devices, per_device(): lax.all_to_all(fock.reshape(16, -1, fock.shape[1]), 'gy', 0, 0, tiled=True)  14.7 us
    all_to_all x2, starting transfers between devices, per_device(): pieces = lax.all_to_all(pieces, 'gy', 0, 0, tiled=True)  14.5 us
    ppermute x2, waiting for transfers between devices, per_device(): far = lax.ppermute(add(mine[1], theirs, 1, far), 'gz', AHEAD)  13.5 us
    ppermute x2, waiting for transfers between devices, per_device(): second = lax.ppermute(first, 'gz', AHEAD)  11.3 us
    ppermute x6, waiting for transfers between devices, per_device(): lax.ppermute(sums, 'gz', [(i, i ^ flip) for i in range(8)])  10 us
  transfers between devices with their start and end apart: 38, of which 18 were waited for; matrix products, arithmetic and copies ran while one was open for 0% of the time, Pallas kernels for 14%

commit v1 on v0

--- a/solution.py
+++ b/solution.py
@@ -99,37 +99,33 @@
     )(mine, theirs, *others)
 
 
-def sums_kernel(place, own, other, gap, fock, message):
+def gram_kernel(own, other, gap, out):
     r, k, _ = own.shape
     gram = jnp.zeros((2 * k, 2 * k), F32)
     scaled = jnp.zeros((2 * k, k), F32)
-    projected = jnp.zeros((2 * k, k), F32)
     for i in range(r):
         both = jnp.concatenate([own[i], other[i]], axis=0)
         gram += dot(both, both, NT)
         high, low = split(own[i].astype(F32) * gap[i : i + 1, :])
         scaled += dot(both, high.astype(BF), NT) + dot(both, low.astype(BF), NT)
-        projected += dot(both, fock[i * k : (i + 1) * k, :], NT)
-    once = jnp.where(place[1] == 0, 1.0, 0.0)
-    projected += once * scaled
-    message[...] = jnp.concatenate([lanes(gram, 2), lanes(projected, 4)], axis=0)
-
-
-def local_sums(place, own, other, gap, fock):
+    out[...] = jnp.concatenate([gram, scaled], axis=1)
+
+
+def gram_parts(own, other, gap):
     k = own.shape[1]
     return pl.pallas_call(
-        sums_kernel,
-        out_shape=array((3 * k // 2, 4 * k), F32),
-        in_specs=[SMEM] + [VMEM] * 4,
+        gram_kernel,
+        out_shape=array((2 * k, 3 * k), F32),
+        in_specs=[VMEM] * 3,
         out_specs=VMEM,
         compiler_params=PARAMS,
-    )(place, own, other, gap, fock)
+    )(own, other, gap)
 
 
 def fock_kernel(place, *refs):
     blocks = refs[:8]
-    b, out, coulomb = refs[8:]
-    r, k, _ = coulomb.shape
+    b, own, other, gram, out, message, coulomb = refs[8:]
+    r, k, _ = own.shape
     rows = r * k
     got = (0, -1, 1, 2)
     order = rows_of(got, place[2], False) + rows_of(got, place[2], True)
@@ -143,22 +139,27 @@
         both = dot(jnp.concatenate([blocks[j][...], fitted], axis=0), b[order[j]], NN)
         total += both[:rows]
         coulomb[order[j]] = both[rows:]
+    projected = jnp.zeros((2 * k, k), F32)
     for i in range(r):
         part = 2.0 * coulomb[i] - total[i * k : (i + 1) * k]
-        out[i * k : (i + 1) * k, :] = part.astype(BF)
-
-
-def fock_parts(place, blocks, b):
-    r, _, n = b.shape
-    rows = blocks[0].shape[0]
+        part = part.astype(BF)
+        out[i * k : (i + 1) * k, :] = part
+        projected += dot(jnp.concatenate([own[i], other[i]], axis=0), part, NT)
+    once = jnp.where(place[1] == 0, 1.0, 0.0)
+    projected += once * gram[:, 2 * k :]
+    message[...] = jnp.concatenate([lanes(gram[:, : 2 * k], 2), lanes(projected, 4)], axis=0)
+
+
+def fock_parts(place, blocks, b, own, other, gram):
+    r, k, n = own.shape
     return pl.pallas_call(
         fock_kernel,
-        out_shape=array((rows, n), BF),
-        in_specs=[SMEM] + [VMEM] * 9,
-        out_specs=VMEM,
-        scratch_shapes=[pltpu.VMEM((r, rows // r, n), F32)],
-        compiler_params=PARAMS,
-    )(place, *blocks, b)
+        out_shape=(array((r * k, n), BF), array((3 * k // 2, 4 * k), F32)),
+        in_specs=[SMEM] + [VMEM] * 12,
+        out_specs=(VMEM, VMEM),
+        scratch_shapes=[pltpu.VMEM((r, k, n), F32)],
+        compiler_params=PARAMS,
+    )(place, *blocks, b, own, other, gram)
 
 
 def owner_kernel(arrived, s0, s1, s2, s3, out, totals):
@@ -268,19 +269,19 @@
         both = jnp.concatenate([own[i], other[i]], axis=0)
         mixed = dot(high, both, TN) + dot(low, both, TN)
         value = (mixed - fock_rows(pieces, i, k, rows)) / gap[i : i + 1, :]
-        out[:, i, :] = value
+        out[i] = value
 
 
 def last_update(place, pieces, inverse, own, other, gap):
     r, k, n = own.shape
     vectors, coupling = pl.pallas_call(
         last_kernel,
-        out_shape=(array((k, r, n), F32), array((k, 2 * k), F32)),
+        out_shape=(array((r, k, n), F32), array((k, 2 * k), F32)),
         in_specs=[SMEM] + [VMEM] * 5,
         out_specs=(VMEM, VMEM),
         compiler_params=PARAMS,
     )(place, pieces, inverse, own, other, gap)
-    return vectors, coupling.T
+    return jnp.transpose(vectors, (1, 0, 2)), coupling.T
 
 
 def ring(step):
@@ -324,8 +325,8 @@
         other = lax.ppermute(own, "gx", OTHER)
         blocks = [first, second, third, fourth, paired]
         blocks += [lax.ppermute(a, "gz", SIBLING) for a in blocks[1:4]]
-        fock = fock_parts(place, blocks, b)
-        sums = local_sums(place, own, other, energy_gap, fock)
+        gram = gram_parts(own, other, energy_gap)
+        fock, sums = fock_parts(place, blocks, b, own, other, gram)
         arrived = lax.all_to_all(
             fock.reshape(16, -1, fock.shape[1]), "gy", 0, 0, tiled=True
         )

time: 194 us -> 191 us (0.985)
  starting transfers between devices: 76.5 us -> 84.7 us
  waiting for transfers between devices: 70.7 us -> 62.6 us
  Pallas kernels: 37.5 us -> 34.9 us
    ppermute x2, waiting for transfers between devices: 0.01 us -> 7.24 us  [per_device(): other = lax.ppermute(own, 'gx', OTHER)]
    ppermute x2, waiting for transfers between devices: 13.5 us -> 8.18 us  [per_device(): far = lax.ppermute(add(mine[1], theirs, 1, far), 'gz', AHEAD)]
    ppermute x2, waiting for transfers between devices: 8.27 us -> 3.74 us  [per_device(): fourth = lax.ppermute(second, 'gz', AHEAD)]
    ppermute x2, starting transfers between devices: 5.13 us -> 9.43 us  [per_device(): second = lax.ppermute(first, 'gz', AHEAD)]
    ppermute x2, starting transfers between devices: 1.64 us -> 5.25 us  [per_device(): other = lax.ppermute(own, 'gx', OTHER)]
    ppermute x2, starting transfers between devices: 4.72 us -> 8.02 us  [per_device(): far = lax.ppermute(add(mine[1], theirs, 1, far), 'gz', AHEAD)]
    ppermute x6, starting transfers between devices: 16.1 us -> 13 us  [per_device(): lax.ppermute(sums, 'gz', [(i, i ^ flip) for i in range(8)])]
    ppermute x6, starting transfers between devices: 1.03 us -> 3.97 us  [per_device(): blocks += [lax.ppermute(a, 'gz', SIBLING) for a in blocks[1:4]]]
  transfers between devices with their start and end apart: 38 -> 38, of which waited for: 18 -> 17; matrix products, arithmetic and copies ran while one was open for 0% -> 0% of each run, Pallas kernels for 14% -> 11%
where the time goes in v1:
time: 191 us; the launch traced here: 190 us
  starting transfers between devices  84.7 us (44%)
  waiting for transfers between devices  62.6 us (33%)
  Pallas kernels  34.9 us (18%)
  local copies, waits for them, and re-layouts  6.93 us (4%)
    ppermute x2, waiting for transfers between devices, per_device(): far = lax.ppermute(add(mine_far, theirs_far, 0), 'gz', AHEAD)  18.4 us
    pallas_call x2, Pallas kernels, inverse_of(): pl.pallas_call(inverse_kernel, out_shape=keep((size, size), F32), in_spec...  16.2 us
    all_to_all x2, starting transfers between devices, per_device(): lax.all_to_all(fock.reshape(16, -1, fock.shape[1]), 'gy', 0, 0, tiled=True)  14.5 us
    all_to_all x2, starting transfers between devices, per_device(): pieces = lax.all_to_all(pieces, 'gy', 0, 0, tiled=True)  14.5 us
    ppermute x6, starting transfers between devices, per_device(): lax.ppermute(sums, 'gz', [(i, i ^ flip) for i in range(8)])  13 us
    ppermute x2, waiting for transfers between devices, per_device(): second = lax.ppermute(first, 'gz', AHEAD)  11.2 us
    ppermute x2, starting transfers between devices, per_device(): second = lax.ppermute(first, 'gz', AHEAD)  9.43 us
    ppermute x6, waiting for transfers between devices, per_device(): lax.ppermute(sums, 'gz', [(i, i ^ flip) for i in range(8)])  9.21 us
  transfers between devices with their start and end apart: 38, of which 17 were waited for; matrix products, arithmetic and copies ran while one was open for 0% of the time, Pallas kernels for 11%

profile of v1, /device:TPU:2, one launch (start us, length us, event | category | flops | bytes accessed | tf_op | source)
XLA Modules:
  0.0 190.1 jit_solution(622773445021343124)
XLA Ops:
  0.6 1.3 copy.13
  2.0 3.0 %copy.12 = bf16[384,8,512]{2,0,1:T(8,128)(2,1)S(1)} copy(bf16[384,8,512]{2,1,0:T(8,128)(2,1)} %param.3) | data formatting | bytes 6291456 | tf_op args[0]
  5.1 1.7 shard_map.50
  6.8 0.1 collective-permute-start
  6.9 1.6 shard_map.52
  8.5 0.6 collective-permute-start.2
  9.1 1.1 collective-permute-done.2.theirs
  10.2 6.4 %collective-permute-start.3 = (bf16[256,384]{1,0:T(8,128)(2,1)S(1)}, bf16[256,384]{1,0:T(8,128)(2,1)S(1)}, u32[]{:S(2)}, u32[]{:S(2)}) collective-permute-start(bf16[256,384]{1,0:T(8,128)(2,1)S(1)} %shard_map.53), channel_id=1, source_target_pairs={{0,6},{1,3},{2,0},{3,5},{4,2},{5,7},{6,4},{7,1},{8,14},{9,11},{10,... | collective-permute-start | bytes 589832 | tf_op jit(solution)/shard_map/ppermute | solution.py:316
  16.7 9.0 %collective-permute-done.3.refs_0_ = bf16[256,384]{1,0:T(8,128)(2,1)S(1)} collective-permute-done((bf16[256,384]{1,0:T(8,128)(2,1)S(1)}, bf16[256,384]{1,0:T(8,128)(2,1)S(1)}, u32[]{:S(2)}, u32[]{:S(2)}) %collective-permute-start.3) | collective-permute-done | bytes 196640 | tf_op jit(solution)/shard_map/ppermute | solution.py:316
  25.8 4.6 %collective-permute-start.4 = (bf16[256,384]{1,0:T(8,128)(2,1)S(1)}, bf16[256,384]{1,0:T(8,128)(2,1)S(1)}, u32[]{:S(2)}, u32[]{:S(2)}) collective-permute-start(bf16[256,384]{1,0:T(8,128)(2,1)S(1)} %shard_map.54), channel_id=1, source_target_pairs={{0,6},{1,3},{2,0},{3,5},{4,2},{5,7},{6,4},{7,1},{8,14},{9,11},{10,... | collective-permute-start | bytes 589832 | tf_op jit(solution)/shard_map/ppermute | solution.py:319
  30.4 4.9 %collective-permute-done.4.refs_1_ = bf16[256,384]{1,0:T(8,128)(2,1)S(1)} collective-permute-done((bf16[256,384]{1,0:T(8,128)(2,1)S(1)}, bf16[256,384]{1,0:T(8,128)(2,1)S(1)}, u32[]{:S(2)}, u32[]{:S(2)}) %collective-permute-start.4) | collective-permute-done | bytes 196640 | tf_op jit(solution)/shard_map/ppermute | solution.py:319
  35.4 4.7 %collective-permute-start.5 = (bf16[256,384]{1,0:T(8,128)(2,1)S(1)}, bf16[256,384]{1,0:T(8,128)(2,1)S(1)}, u32[]{:S(2)}, u32[]{:S(2)}) collective-permute-start(bf16[256,384]{1,0:T(8,128)(2,1)S(1)} %shard_map.55.refs_0_), channel_id=1, source_target_pairs={{0,6},{1,3},{2,0},{3,5},{4,2},{5,7},{6,4},{7,1},{8,14},{9,11},{10,... | collective-permute-start | bytes 589832 | tf_op jit(solution)/shard_map/ppermute | solution.py:321
  40.1 5.1 %collective-permute-done.5.refs_1_ = bf16[256,384]{1,0:T(8,128)(2,1)S(1)} collective-permute-done((bf16[256,384]{1,0:T(8,128)(2,1)S(1)}, bf16[256,384]{1,0:T(8,128)(2,1)S(1)}, u32[]{:S(2)}, u32[]{:S(2)}) %collective-permute-start.5) | collective-permute-done | bytes 196640 | tf_op jit(solution)/shard_map/ppermute | solution.py:321
  45.2 2.8 %collective-permute-start.7 = (bf16[256,384]{1,0:T(8,128)(2,1)S(1)}, bf16[256,384]{1,0:T(8,128)(2,1)S(1)}, u32[]{:S(2)}, u32[]{:S(2)}) collective-permute-start(bf16[256,384]{1,0:T(8,128)(2,1)S(1)} %collective-permute-done.5.refs_1_), channel_id=1, source_target_pairs={{0,6},{1,3},{2,0},{3,5},{4,2},{5,7},{6,4},{7,1},{8,14},{9,11},{10,... | collective-permute-start | bytes 589832 | tf_op jit(solution)/shard_map/ppermute | solution.py:324
  48.0 5.2 %collective-permute-start.12 = (bf16[8,32,512]{2,1,0:T(8,128)(2,1)S(1)}, bf16[8,32,512]{2,1,0:T(8,128)(2,1)S(1)}, u32[]{:S(2)}, u32[]{:S(2)}) collective-permute-start(bf16[8,32,512]{2,1,0:T(8,128)(2,1)S(1)} %bitcast.21), channel_id=1, source_target_pairs={{0,128},{128,0},{1,129},{129,1},{2,130},{130,2},{3,131},{131,3},{4... | collective-permute-start | bytes 786440 | tf_op jit(solution)/shard_map/ppermute | solution.py:325
  53.3 0.5 collective-permute-start.9
  53.8 0.5 collective-permute-start.11
  54.3 5.4 %collective-permute-done.12.other.refs_10_ = bf16[8,32,512]{2,1,0:T(8,128)(2,1)S(1)} collective-permute-done((bf16[8,32,512]{2,1,0:T(8,128)(2,1)S(1)}, bf16[8,32,512]{2,1,0:T(8,128)(2,1)S(1)}, u32[]{:S(2)}, u32[]{:S(2)}) %collective-permute-start.12) | collective-permute-done | bytes 262176 | tf_op jit(solution)/shard_map/ppermute | solution.py:325
  59.7 0.6 shard_map.56.refs_11_
  60.4 2.3 %shard_map.57 = (bf16[256,512]{1,0:T(8,128)(2,1)S(1)}, f32[48,128]{1,0:T(8,128)S(1)}) custom-call(s32[3]{0:T(128)S(1)} %pad_add_fusion.refs_0_.place, bf16[256,384]{1,0:T(8,128)(2,1)S(1)} %shard_map.55.refs_0_, bf16[256,384]{1,0:T(8,128)(2,1)S(1)} %collective-permute-done.5.refs_1_, bf16[256,384]{1,0:T(8,128)(2,1)S(1)} %collective-permute-done.6.refs_2_, ...), custom_call_target="tpu_custom_call" | custom-call | tf_op jit(solution)/shard_map/pallas_call | solution.py:155
  62.7 0.7 copy-done.6
  63.4 7.3 %all-to-all-start = ((bf16[16,16,512]{2,1,0:T(8,128)(2,1)}), bf16[16,16,512]{2,1,0:T(8,128)(2,1)S(1)}, u32[]{:S(2)}, u32[]{:S(2)}) async-start(bf16[16,16,512]{2,1,0:T(8,128)(2,1)} %bitcast.26), calls=%async_computation | async-start | bytes 524288 | tf_op jit(solution)/shard_map/all_to_all | solution.py:330
  70.7 1.2 collective-permute-done.13
  71.9 1.1 collective-permute-start.14
  73.0 3.0 %collective-permute-start.15 = (f32[48,128]{1,0:T(8,128)S(1)}, f32[48,128]{1,0:T(8,128)S(1)}, u32[]{:S(2)}, u32[]{:S(2)}) collective-permute-start(f32[48,128]{1,0:T(8,128)S(1)} %add.6.s0), channel_id=1, source_target_pairs={{0,4},{1,5},{2,6},{3,7},{4,0},{5,1},{6,2},{7,3},{8,12},{9,13},{10,... | collective-permute-start | bytes 73736 | tf_op jit(solution)/shard_map/ppermute | solution.py:335
  76.0 2.4 %collective-permute-start.16 = (f32[48,128]{1,0:T(8,128)S(1)}, f32[48,128]{1,0:T(8,128)S(1)}, u32[]{:S(2)}, u32[]{:S(2)}) collective-permute-start(f32[48,128]{1,0:T(8,128)S(1)} %add.6.s0), channel_id=1, source_target_pairs={{0,6},{1,7},{2,4},{3,5},{4,2},{5,3},{6,0},{7,1},{8,14},{9,15},{10,... | collective-permute-start | bytes 73736 | tf_op jit(solution)/shard_map/ppermute | solution.py:335
  78.4 2.5 %collective-permute-done.15.s2 = f32[48,128]{1,0:T(8,128)S(1)} collective-permute-done((f32[48,128]{1,0:T(8,128)S(1)}, f32[48,128]{1,0:T(8,128)S(1)}, u32[]{:S(2)}, u32[]{:S(2)}) %collective-permute-start.15) | collective-permute-done | bytes 24608 | tf_op jit(solution)/shard_map/ppermute | solution.py:335
  80.9 1.1 collective-permute-done.16.s3
  82.0 0.6 shard_map.58
  82.6 0.7 copy-done.4
  83.3 7.2 %all-to-all-start.1 = ((bf16[16,96,128]{2,1,0:T(8,128)(2,1)}), bf16[16,96,128]{2,1,0:T(8,128)(2,1)}, u32[]{:S(2)}, u32[]{:S(2)}) async-start(bf16[16,96,128]{2,1,0:T(8,128)(2,1)} %copy-done.4), calls=%async_computation.1 | async-start | bytes 786432 | tf_op jit(solution)/shard_map/all_to_all | solution.py:341
  90.6 8.8 %shard_map.59.inverse = f32[64,64]{1,0:T(8,128)} custom-call(f32[32,128]{1,0:T(8,128)} %get-tuple-element.33.totals), custom_call_target="tpu_custom_call" | custom-call | tf_op jit(solution)/shard_map/pallas_call | solution.py:214
  99.3 1.8 shard_map.60.refs_1_.own.refs_9_
  101.1 1.7 shard_map.61
  102.8 0.1 collective-permute-start.17
  102.9 1.6 shard_map.63
  104.5 0.6 collective-permute-start.19
  105.1 1.1 collective-permute-done.19.theirs
  106.2 2.5 %collective-permute-start.20 = (bf16[256,384]{1,0:T(8,128)(2,1)S(1)}, bf16[256,384]{1,0:T(8,128)(2,1)S(1)}, u32[]{:S(2)}, u32[]{:S(2)}) collective-permute-start(bf16[256,384]{1,0:T(8,128)(2,1)S(1)} %shard_map.64), channel_id=1, source_target_pairs={{0,6},{1,3},{2,0},{3,5},{4,2},{5,7},{6,4},{7,1},{8,14},{9,11},{10,... | collective-permute-start | bytes 589832 | tf_op jit(solution)/shard_map/ppermute | solution.py:316
  108.7 0.6 collective-permute-start.18
  109.4 9.5 %collective-permute-done.20.refs_0_ = bf16[256,384]{1,0:T(8,128)(2,1)S(1)} collective-permute-done((bf16[256,384]{1,0:T(8,128)(2,1)S(1)}, bf16[256,384]{1,0:T(8,128)(2,1)S(1)}, u32[]{:S(2)}, u32[]{:S(2)}) %collective-permute-start.20) | collective-permute-done | bytes 196640 | tf_op jit(solution)/shard_map/ppermute | solution.py:316
  118.9 3.4 %collective-permute-start.21 = (bf16[256,384]{1,0:T(8,128)(2,1)S(1)}, bf16[256,384]{1,0:T(8,128)(2,1)S(1)}, u32[]{:S(2)}, u32[]{:S(2)}) collective-permute-start(bf16[256,384]{1,0:T(8,128)(2,1)S(1)} %shard_map.65), channel_id=1, source_target_pairs={{0,6},{1,3},{2,0},{3,5},{4,2},{5,7},{6,4},{7,1},{8,14},{9,11},{10,... | collective-permute-start | bytes 589832 | tf_op jit(solution)/shard_map/ppermute | solution.py:319
  122.3 3.3 %collective-permute-done.21.refs_1_ = bf16[256,384]{1,0:T(8,128)(2,1)S(1)} collective-permute-done((bf16[256,384]{1,0:T(8,128)(2,1)S(1)}, bf16[256,384]{1,0:T(8,128)(2,1)S(1)}, u32[]{:S(2)}, u32[]{:S(2)}) %collective-permute-start.21) | collective-permute-done | bytes 196640 | tf_op jit(solution)/shard_map/ppermute | solution.py:319
  125.6 4.7 %collective-permute-start.22 = (bf16[256,384]{1,0:T(8,128)(2,1)S(1)}, bf16[256,384]{1,0:T(8,128)(2,1)S(1)}, u32[]{:S(2)}, u32[]{:S(2)}) collective-permute-start(bf16[256,384]{1,0:T(8,128)(2,1)S(1)} %shard_map.66.refs_0_), channel_id=1, source_target_pairs={{0,6},{1,3},{2,0},{3,5},{4,2},{5,7},{6,4},{7,1},{8,14},{9,11},{10,... | collective-permute-start | bytes 589832 | tf_op jit(solution)/shard_map/ppermute | solution.py:321
  130.3 6.2 %collective-permute-done.22.refs_1_ = bf16[256,384]{1,0:T(8,128)(2,1)S(1)} collective-permute-done((bf16[256,384]{1,0:T(8,128)(2,1)S(1)}, bf16[256,384]{1,0:T(8,128)(2,1)S(1)}, u32[]{:S(2)}, u32[]{:S(2)}) %collective-permute-start.22) | collective-permute-done | bytes 196640 | tf_op jit(solution)/shard_map/ppermute | solution.py:321
  136.5 2.4 %collective-permute-start.24 = (bf16[256,384]{1,0:T(8,128)(2,1)S(1)}, bf16[256,384]{1,0:T(8,128)(2,1)S(1)}, u32[]{:S(2)}, u32[]{:S(2)}) collective-permute-start(bf16[256,384]{1,0:T(8,128)(2,1)S(1)} %collective-permute-done.22.refs_1_), channel_id=1, source_target_pairs={{0,6},{1,3},{2,0},{3,5},{4,2},{5,7},{6,4},{7,1},{8,14},{9,11},{10,... | collective-permute-start | bytes 589832 | tf_op jit(solution)/shard_map/ppermute | solution.py:324
  138.9 0.5 collective-permute-start.26
  139.4 3.7 %collective-permute-done.24.refs_3_ = bf16[256,384]{1,0:T(8,128)(2,1)S(1)} collective-permute-done((bf16[256,384]{1,0:T(8,128)(2,1)S(1)}, bf16[256,384]{1,0:T(8,128)(2,1)S(1)}, u32[]{:S(2)}, u32[]{:S(2)}) %collective-permute-start.24) | collective-permute-done | bytes 196640 | tf_op jit(solution)/shard_map/ppermute | solution.py:324
  143.2 2.4 %collective-permute-start.28 = (bf16[256,384]{1,0:T(8,128)(2,1)S(1)}, bf16[256,384]{1,0:T(8,128)(2,1)S(1)}, u32[]{:S(2)}, u32[]{:S(2)}) collective-permute-start(bf16[256,384]{1,0:T(8,128)(2,1)S(1)} %collective-permute-done.24.refs_3_), channel_id=1, source_target_pairs={{0,1},{1,0},{2,3},{3,2},{4,5},{5,4},{6,7},{7,6},{8,9},{9,8},{10,11... | collective-permute-start | bytes 589832 | tf_op jit(solution)/shard_map/ppermute | solution.py:327
  145.6 1.8 collective-permute-done.29.other.refs_10_
  147.4 0.6 shard_map.67.refs_11_
  148.1 2.7 %shard_map.68 = (bf16[256,512]{1,0:T(8,128)(2,1)}, f32[48,128]{1,0:T(8,128)S(1)}) custom-call(s32[3]{0:T(128)S(1)} %pad_add_fusion.refs_0_.place, bf16[256,384]{1,0:T(8,128)(2,1)S(1)} %shard_map.66.refs_0_, bf16[256,384]{1,0:T(8,128)(2,1)S(1)} %collective-permute-done.22.refs_1_, bf16[256,384]{1,0:T(8,128)(2,1)S(1)} %collective-permute-done.23.refs_2_, ...), custom_call_target="tpu_custom_call" | custom-call | tf_op jit(solution)/shard_map/pallas_call | solution.py:155
  150.8 7.2 %all-to-all-start.2 = ((bf16[16,16,512]{2,1,0:T(8,128)(2,1)}), bf16[16,16,512]{2,1,0:T(8,128)(2,1)S(1)}, u32[]{:S(2)}, u32[]{:S(2)}) async-start(bf16[16,16,512]{2,1,0:T(8,128)(2,1)} %bitcast.6), calls=%async_computation.2 | async-start | bytes 524288 | tf_op jit(solution)/shard_map/all_to_all | solution.py:330
  158.1 1.2 collective-permute-done.30
  159.3 0.5 collective-permute-start.31
  159.8 5.7 %collective-permute-start.32 = (f32[48,128]{1,0:T(8,128)S(1)}, f32[48,128]{1,0:T(8,128)S(1)}, u32[]{:S(2)}, u32[]{:S(2)}) collective-permute-start(f32[48,128]{1,0:T(8,128)S(1)} %add.7.s0), channel_id=1, source_target_pairs={{0,4},{1,5},{2,6},{3,7},{4,0},{5,1},{6,2},{7,3},{8,12},{9,13},{10,... | collective-permute-start | bytes 73736 | tf_op jit(solution)/shard_map/ppermute | solution.py:335
  165.5 0.3 collective-permute-start.33
  165.8 1.8 collective-permute-done.32.s2
  167.6 3.9 %collective-permute-done.33.s3 = f32[48,128]{1,0:T(8,128)S(1)} collective-permute-done((f32[48,128]{1,0:T(8,128)S(1)}, f32[48,128]{1,0:T(8,128)S(1)}, u32[]{:S(2)}, u32[]{:S(2)}) %collective-permute-start.33) | collective-permute-done | bytes 24608 | tf_op jit(solution)/shard_map/ppermute | solution.py:335
  171.4 0.8 shard_map.69
  172.2 7.2 %all-to-all-start.3 = ((bf16[16,96,128]{2,1,0:T(8,128)(2,1)}), bf16[16,96,128]{2,1,0:T(8,128)(2,1)S(1)}, u32[]{:S(2)}, u32[]{:S(2)}) async-start(bf16[16,96,128]{2,1,0:T(8,128)(2,1)} %get-tuple-element.42), calls=%async_computation.3 | async-start | bytes 786432 | tf_op jit(solution)/shard_map/all_to_all | solution.py:341
  179.5 7.4 %shard_map.70.inverse = f32[64,64]{1,0:T(8,128)S(1)} custom-call(f32[32,128]{1,0:T(8,128)S(1)} %get-tuple-element.43.totals), custom_call_target="tpu_custom_call" | custom-call | tf_op jit(solution)/shard_map/pallas_call | solution.py:214
  186.9 2.1 %shard_map.71 = (f32[8,32,512]{2,1,0:T(8,128)S(1)}, f32[32,64]{1,0:T(8,128)}) custom-call(s32[3]{0:T(128)S(1)} %pad_add_fusion.refs_0_.place, bf16[16,96,128]{2,1,0:T(8,128)(2,1)S(1)} %all-to-all-done.3.pieces, f32[64,64]{1,0:T(8,128)S(1)} %shard_map.70.inverse, bf16[8,32,512]{2,1,0:T(8,128)(2,1)} %copy-done, bf16[8,32,512]{2,1,0:T(8,128)(2,1)} %copy-done.2, ...), custom_call_target="tpu_custom_call" | custom-call | tf_op jit(solution)/shard_map/pallas_call | solution.py:277
  189.0 1.1 copy.7
  (54 shorter events, 0.7 us)
Async XLA Ops:
  2.0 58.4 %copy-start.1 = (bf16[32,8,512]{2,0,1:T(8,128)(2,1)}, bf16[32,8,512]{2,0,1:T(8,128)(2,1)S(1)}, u32[]{:S(2)}) copy-start(bf16[32,8,512]{2,0,1:T(8,128)(2,1)S(1)} %copy.13) | copy-start | bytes 786436
  6.8 9.8 %collective-permute-start = (bf16[3,256,384]{2,1,0:T(8,128)(2,1)S(1)}, bf16[3,256,384]{2,1,0:T(8,128)(2,1)S(1)}, u32[]{:S(2)}, u32[]{:S(2)}) collective-permute-start(bf16[3,256,384]{2,1,0:T(8,128)(2,1)S(1)} %get-tuple-element.25), channel_id=1, source_target_pairs={{0,1},{1,0},{2,3},{3,2},{4,5},{5,4},{6,7},{7,6},{8,9},{9,8},{10,11... | collective-permute-start | bytes 1769480 | tf_op jit(solution)/shard_map/ppermute | solution.py:317
  8.5 51.2 %copy-start.5 = (f32[8,512]{1,0:T(8,128)S(1)}, f32[8,512]{1,0:T(8,128)}, u32[]{:S(2)}) copy-start(f32[8,512]{1,0:T(8,128)} %gap.7) | copy-start | bytes 49156
  8.5 1.7 collective-permute-start.2
  10.2 15.5 %collective-permute-start.3 = (bf16[256,384]{1,0:T(8,128)(2,1)S(1)}, bf16[256,384]{1,0:T(8,128)(2,1)S(1)}, u32[]{:S(2)}, u32[]{:S(2)}) collective-permute-start(bf16[256,384]{1,0:T(8,128)(2,1)S(1)} %shard_map.53), channel_id=1, source_target_pairs={{0,6},{1,3},{2,0},{3,5},{4,2},{5,7},{6,4},{7,1},{8,14},{9,11},{10,... | collective-permute-start | bytes 589832 | tf_op jit(solution)/shard_map/ppermute | solution.py:316
  16.6 13.8 %collective-permute-start.1 = (bf16[256,384]{1,0:T(8,128)(2,1)S(1)}, bf16[256,384]{1,0:T(8,128)(2,1)S(1)}, u32[]{:S(2)}, u32[]{:S(2)}) collective-permute-start(bf16[256,384]{1,0:T(8,128)(2,1)S(1)} %shard_map.51), channel_id=1, source_target_pairs={{0,2},{1,7},{2,4},{3,1},{4,6},{5,3},{6,0},{7,5},{8,10},{9,15},{10,... | collective-permute-start | bytes 589832 | tf_op jit(solution)/shard_map/ppermute | solution.py:318
  25.8 9.6 %collective-permute-start.4 = (bf16[256,384]{1,0:T(8,128)(2,1)S(1)}, bf16[256,384]{1,0:T(8,128)(2,1)S(1)}, u32[]{:S(2)}, u32[]{:S(2)}) collective-permute-start(bf16[256,384]{1,0:T(8,128)(2,1)S(1)} %shard_map.54), channel_id=1, source_target_pairs={{0,6},{1,3},{2,0},{3,5},{4,2},{5,7},{6,4},{7,1},{8,14},{9,11},{10,... | collective-permute-start | bytes 589832 | tf_op jit(solution)/shard_map/ppermute | solution.py:319
  35.4 9.8 %collective-permute-start.5 = (bf16[256,384]{1,0:T(8,128)(2,1)S(1)}, bf16[256,384]{1,0:T(8,128)(2,1)S(1)}, u32[]{:S(2)}, u32[]{:S(2)}) collective-permute-start(bf16[256,384]{1,0:T(8,128)(2,1)S(1)} %shard_map.55.refs_0_), channel_id=1, source_target_pairs={{0,6},{1,3},{2,0},{3,5},{4,2},{5,7},{6,4},{7,1},{8,14},{9,11},{10,... | collective-permute-start | bytes 589832 | tf_op jit(solution)/shard_map/ppermute | solution.py:321
  40.1 13.6 %collective-permute-start.6 = (bf16[256,384]{1,0:T(8,128)(2,1)S(1)}, bf16[256,384]{1,0:T(8,128)(2,1)S(1)}, u32[]{:S(2)}, u32[]{:S(2)}) collective-permute-start(bf16[256,384]{1,0:T(8,128)(2,1)S(1)} %shard_map.55.refs_0_), channel_id=1, source_target_pairs={{0,2},{1,7},{2,4},{3,1},{4,6},{5,3},{6,0},{7,5},{8,10},{9,15},{10,... | collective-permute-start | bytes 589832 | tf_op jit(solution)/shard_map/ppermute | solution.py:323
  45.2 8.6 %collective-permute-start.7 = (bf16[256,384]{1,0:T(8,128)(2,1)S(1)}, bf16[256,384]{1,0:T(8,128)(2,1)S(1)}, u32[]{:S(2)}, u32[]{:S(2)}) collective-permute-start(bf16[256,384]{1,0:T(8,128)(2,1)S(1)} %collective-permute-done.5.refs_1_), channel_id=1, source_target_pairs={{0,6},{1,3},{2,0},{3,5},{4,2},{5,7},{6,4},{7,1},{8,14},{9,11},{10,... | collective-permute-start | bytes 589832 | tf_op jit(solution)/shard_map/ppermute | solution.py:324
  48.0 11.7 %collective-permute-start.12 = (bf16[8,32,512]{2,1,0:T(8,128)(2,1)S(1)}, bf16[8,32,512]{2,1,0:T(8,128)(2,1)S(1)}, u32[]{:S(2)}, u32[]{:S(2)}) collective-permute-start(bf16[8,32,512]{2,1,0:T(8,128)(2,1)S(1)} %bitcast.21), channel_id=1, source_target_pairs={{0,128},{128,0},{1,129},{129,1},{2,130},{130,2},{3,131},{131,3},{4... | collective-permute-start | bytes 786440 | tf_op jit(solution)/shard_map/ppermute | solution.py:325
  53.3 7.1 %collective-permute-start.8 = (bf16[256,384]{1,0:T(8,128)(2,1)S(1)}, bf16[256,384]{1,0:T(8,128)(2,1)S(1)}, u32[]{:S(2)}, u32[]{:S(2)}) collective-permute-start(bf16[256,384]{1,0:T(8,128)(2,1)S(1)} %shard_map.55.refs_0_), channel_id=1, source_target_pairs={{0,1},{1,0},{2,3},{3,2},{4,5},{5,4},{6,7},{7,6},{8,9},{9,8},{10,11... | collective-permute-start | bytes 589832 | tf_op jit(solution)/shard_map/ppermute | solution.py:322
  53.3 7.1 %collective-permute-start.9 = (bf16[256,384]{1,0:T(8,128)(2,1)S(1)}, bf16[256,384]{1,0:T(8,128)(2,1)S(1)}, u32[]{:S(2)}, u32[]{:S(2)}) collective-permute-start(bf16[256,384]{1,0:T(8,128)(2,1)S(1)} %collective-permute-done.5.refs_1_), channel_id=1, source_target_pairs={{0,1},{1,0},{2,3},{3,2},{4,5},{5,4},{6,7},{7,6},{8,9},{9,8},{10,11... | collective-permute-start | bytes 589832 | tf_op jit(solution)/shard_map/ppermute | solution.py:327
  53.8 6.6 %collective-permute-start.10 = (bf16[256,384]{1,0:T(8,128)(2,1)S(1)}, bf16[256,384]{1,0:T(8,128)(2,1)S(1)}, u32[]{:S(2)}, u32[]{:S(2)}) collective-permute-start(bf16[256,384]{1,0:T(8,128)(2,1)S(1)} %collective-permute-done.6.refs_2_), channel_id=1, source_target_pairs={{0,1},{1,0},{2,3},{3,2},{4,5},{5,4},{6,7},{7,6},{8,9},{9,8},{10,11... | collective-permute-start | bytes 589832 | tf_op jit(solution)/shard_map/ppermute | solution.py:327
  53.8 6.6 %collective-permute-start.11 = (bf16[256,384]{1,0:T(8,128)(2,1)S(1)}, bf16[256,384]{1,0:T(8,128)(2,1)S(1)}, u32[]{:S(2)}, u32[]{:S(2)}) collective-permute-start(bf16[256,384]{1,0:T(8,128)(2,1)S(1)} %collective-permute-done.7.refs_3_), channel_id=1, source_target_pairs={{0,1},{1,0},{2,3},{3,2},{4,5},{5,4},{6,7},{7,6},{8,9},{9,8},{10,11... | collective-permute-start | bytes 589832 | tf_op jit(solution)/shard_map/ppermute | solution.py:327
  59.7 3.0 %copy-start.3 = (bf16[8,32,512]{2,1,0:T(8,128)(2,1)}, bf16[8,32,512]{2,1,0:T(8,128)(2,1)S(1)}, u32[]{:S(2)}) copy-start(bf16[8,32,512]{2,1,0:T(8,128)(2,1)S(1)} %collective-permute-done.12.other.refs_10_) | copy-start | bytes 786436
  62.7 0.7 copy-start.6
  63.4 18.5 %all-to-all-start = ((bf16[16,16,512]{2,1,0:T(8,128)(2,1)}), bf16[16,16,512]{2,1,0:T(8,128)(2,1)S(1)}, u32[]{:S(2)}, u32[]{:S(2)}) async-start(bf16[16,16,512]{2,1,0:T(8,128)(2,1)} %bitcast.26), calls=%async_computation | async-start | bytes 524288 | tf_op jit(solution)/shard_map/all_to_all | solution.py:330
  70.7 1.2 collective-permute-start.13
  71.9 6.5 %collective-permute-start.14 = (f32[48,128]{1,0:T(8,128)S(1)}, f32[48,128]{1,0:T(8,128)S(1)}, u32[]{:S(2)}, u32[]{:S(2)}) collective-permute-start(f32[48,128]{1,0:T(8,128)S(1)} %add.6.s0), channel_id=1, source_target_pairs={{0,2},{1,3},{2,0},{3,1},{4,6},{5,7},{6,4},{7,5},{8,10},{9,11},{10,... | collective-permute-start | bytes 73736 | tf_op jit(solution)/shard_map/ppermute | solution.py:335
  73.0 7.9 %collective-permute-start.15 = (f32[48,128]{1,0:T(8,128)S(1)}, f32[48,128]{1,0:T(8,128)S(1)}, u32[]{:S(2)}, u32[]{:S(2)}) collective-permute-start(f32[48,128]{1,0:T(8,128)S(1)} %add.6.s0), channel_id=1, source_target_pairs={{0,4},{1,5},{2,6},{3,7},{4,0},{5,1},{6,2},{7,3},{8,12},{9,13},{10,... | collective-permute-start | bytes 73736 | tf_op jit(solution)/shard_map/ppermute | solution.py:335
  76.0 5.9 %collective-permute-start.16 = (f32[48,128]{1,0:T(8,128)S(1)}, f32[48,128]{1,0:T(8,128)S(1)}, u32[]{:S(2)}, u32[]{:S(2)}) collective-permute-start(f32[48,128]{1,0:T(8,128)S(1)} %add.6.s0), channel_id=1, source_target_pairs={{0,6},{1,7},{2,4},{3,5},{4,2},{5,3},{6,0},{7,1},{8,14},{9,15},{10,... | collective-permute-start | bytes 73736 | tf_op jit(solution)/shard_map/ppermute | solution.py:335
  82.6 0.7 copy-start.4
  83.3 16.0 %all-to-all-start.1 = ((bf16[16,96,128]{2,1,0:T(8,128)(2,1)}), bf16[16,96,128]{2,1,0:T(8,128)(2,1)}, u32[]{:S(2)}, u32[]{:S(2)}) async-start(bf16[16,96,128]{2,1,0:T(8,128)(2,1)} %copy-done.4), calls=%async_computation.1 | async-start | bytes 786432 | tf_op jit(solution)/shard_map/all_to_all | solution.py:341
  101.1 47.0 %copy-start = (bf16[8,32,512]{2,1,0:T(8,128)(2,1)}, bf16[8,32,512]{2,1,0:T(8,128)(2,1)S(1)}, u32[]{:S(2)}) copy-start(bf16[8,32,512]{2,1,0:T(8,128)(2,1)S(1)} %shard_map.60.refs_1_.own.refs_9_) | copy-start | bytes 786436
  102.8 5.9 %collective-permute-start.17 = (bf16[3,256,384]{2,1,0:T(8,128)(2,1)S(1)}, bf16[3,256,384]{2,1,0:T(8,128)(2,1)S(1)}, u32[]{:S(2)}, u32[]{:S(2)}) collective-permute-start(bf16[3,256,384]{2,1,0:T(8,128)(2,1)S(1)} %get-tuple-element.35), channel_id=1, source_target_pairs={{0,1},{1,0},{2,3},{3,2},{4,5},{5,4},{6,7},{7,6},{8,9},{9,8},{10,11... | collective-permute-start | bytes 1769480 | tf_op jit(solution)/shard_map/ppermute | solution.py:317
  104.5 1.7 collective-permute-start.19
  106.2 12.6 %collective-permute-start.20 = (bf16[256,384]{1,0:T(8,128)(2,1)S(1)}, bf16[256,384]{1,0:T(8,128)(2,1)S(1)}, u32[]{:S(2)}, u32[]{:S(2)}) collective-permute-start(bf16[256,384]{1,0:T(8,128)(2,1)S(1)} %shard_map.64), channel_id=1, source_target_pairs={{0,6},{1,3},{2,0},{3,5},{4,2},{5,7},{6,4},{7,1},{8,14},{9,11},{10,... | collective-permute-start | bytes 589832 | tf_op jit(solution)/shard_map/ppermute | solution.py:316
  108.7 13.6 %collective-permute-start.18 = (bf16[256,384]{1,0:T(8,128)(2,1)S(1)}, bf16[256,384]{1,0:T(8,128)(2,1)S(1)}, u32[]{:S(2)}, u32[]{:S(2)}) collective-permute-start(bf16[256,384]{1,0:T(8,128)(2,1)S(1)} %shard_map.62), channel_id=1, source_target_pairs={{0,2},{1,7},{2,4},{3,1},{4,6},{5,3},{6,0},{7,5},{8,10},{9,15},{10,... | collective-permute-start | bytes 589832 | tf_op jit(solution)/shard_map/ppermute | solution.py:318
  118.9 6.6 %collective-permute-start.21 = (bf16[256,384]{1,0:T(8,128)(2,1)S(1)}, bf16[256,384]{1,0:T(8,128)(2,1)S(1)}, u32[]{:S(2)}, u32[]{:S(2)}) collective-permute-start(bf16[256,384]{1,0:T(8,128)(2,1)S(1)} %shard_map.65), channel_id=1, source_target_pairs={{0,6},{1,3},{2,0},{3,5},{4,2},{5,7},{6,4},{7,1},{8,14},{9,11},{10,... | collective-permute-start | bytes 589832 | tf_op jit(solution)/shard_map/ppermute | solution.py:319
  125.6 10.9 %collective-permute-start.22 = (bf16[256,384]{1,0:T(8,128)(2,1)S(1)}, bf16[256,384]{1,0:T(8,128)(2,1)S(1)}, u32[]{:S(2)}, u32[]{:S(2)}) collective-permute-start(bf16[256,384]{1,0:T(8,128)(2,1)S(1)} %shard_map.66.refs_0_), channel_id=1, source_target_pairs={{0,6},{1,3},{2,0},{3,5},{4,2},{5,7},{6,4},{7,1},{8,14},{9,11},{10,... | collective-permute-start | bytes 589832 | tf_op jit(solution)/shard_map/ppermute | solution.py:321
  130.3 9.1 %collective-permute-start.23 = (bf16[256,384]{1,0:T(8,128)(2,1)S(1)}, bf16[256,384]{1,0:T(8,128)(2,1)S(1)}, u32[]{:S(2)}, u32[]{:S(2)}) collective-permute-start(bf16[256,384]{1,0:T(8,128)(2,1)S(1)} %shard_map.66.refs_0_), channel_id=1, source_target_pairs={{0,2},{1,7},{2,4},{3,1},{4,6},{5,3},{6,0},{7,5},{8,10},{9,15},{10,... | collective-permute-start | bytes 589832 | tf_op jit(solution)/shard_map/ppermute | solution.py:323
  136.5 6.7 %collective-permute-start.24 = (bf16[256,384]{1,0:T(8,128)(2,1)S(1)}, bf16[256,384]{1,0:T(8,128)(2,1)S(1)}, u32[]{:S(2)}, u32[]{:S(2)}) collective-permute-start(bf16[256,384]{1,0:T(8,128)(2,1)S(1)} %collective-permute-done.22.refs_1_), channel_id=1, source_target_pairs={{0,6},{1,3},{2,0},{3,5},{4,2},{5,7},{6,4},{7,1},{8,14},{9,11},{10,... | collective-permute-start | bytes 589832 | tf_op jit(solution)/shard_map/ppermute | solution.py:324
  138.9 8.5 %collective-permute-start.29 = (bf16[8,32,512]{2,1,0:T(8,128)(2,1)S(1)}, bf16[8,32,512]{2,1,0:T(8,128)(2,1)S(1)}, u32[]{:S(2)}, u32[]{:S(2)}) collective-permute-start(bf16[8,32,512]{2,1,0:T(8,128)(2,1)S(1)} %shard_map.60.refs_1_.own.refs_9_), channel_id=1, source_target_pairs={{0,128},{128,0},{1,129},{129,1},{2,130},{130,2},{3,131},{131,3},{4... | collective-permute-start | bytes 786440 | tf_op jit(solution)/shard_map/ppermute | solution.py:325
  138.9 9.1 %collective-permute-start.25 = (bf16[256,384]{1,0:T(8,128)(2,1)S(1)}, bf16[256,384]{1,0:T(8,128)(2,1)S(1)}, u32[]{:S(2)}, u32[]{:S(2)}) collective-permute-start(bf16[256,384]{1,0:T(8,128)(2,1)S(1)} %shard_map.66.refs_0_), channel_id=1, source_target_pairs={{0,1},{1,0},{2,3},{3,2},{4,5},{5,4},{6,7},{7,6},{8,9},{9,8},{10,11... | collective-permute-start | bytes 589832 | tf_op jit(solution)/shard_map/ppermute | solution.py:322
  138.9 9.1 %collective-permute-start.26 = (bf16[256,384]{1,0:T(8,128)(2,1)S(1)}, bf16[256,384]{1,0:T(8,128)(2,1)S(1)}, u32[]{:S(2)}, u32[]{:S(2)}) collective-permute-start(bf16[256,384]{1,0:T(8,128)(2,1)S(1)} %collective-permute-done.22.refs_1_), channel_id=1, source_target_pairs={{0,1},{1,0},{2,3},{3,2},{4,5},{5,4},{6,7},{7,6},{8,9},{9,8},{10,11... | collective-permute-start | bytes 589832 | tf_op jit(solution)/shard_map/ppermute | solution.py:327
  139.4 8.6 %collective-permute-start.27 = (bf16[256,384]{1,0:T(8,128)(2,1)S(1)}, bf16[256,384]{1,0:T(8,128)(2,1)S(1)}, u32[]{:S(2)}, u32[]{:S(2)}) collective-permute-start(bf16[256,384]{1,0:T(8,128)(2,1)S(1)} %collective-permute-done.23.refs_2_), channel_id=1, source_target_pairs={{0,1},{1,0},{2,3},{3,2},{4,5},{5,4},{6,7},{7,6},{8,9},{9,8},{10,11... | collective-permute-start | bytes 589832 | tf_op jit(solution)/shard_map/ppermute | solution.py:327
  143.2 4.9 %collective-permute-start.28 = (bf16[256,384]{1,0:T(8,128)(2,1)S(1)}, bf16[256,384]{1,0:T(8,128)(2,1)S(1)}, u32[]{:S(2)}, u32[]{:S(2)}) collective-permute-start(bf16[256,384]{1,0:T(8,128)(2,1)S(1)} %collective-permute-done.24.refs_3_), channel_id=1, source_target_pairs={{0,1},{1,0},{2,3},{3,2},{4,5},{5,4},{6,7},{7,6},{8,9},{9,8},{10,11... | collective-permute-start | bytes 589832 | tf_op jit(solution)/shard_map/ppermute | solution.py:327
  147.4 3.4 %copy-start.2 = (bf16[8,32,512]{2,1,0:T(8,128)(2,1)}, bf16[8,32,512]{2,1,0:T(8,128)(2,1)S(1)}, u32[]{:S(2)}) copy-start(bf16[8,32,512]{2,1,0:T(8,128)(2,1)S(1)} %collective-permute-done.29.other.refs_10_) | copy-start | bytes 786436
  150.8 20.6 %all-to-all-start.2 = ((bf16[16,16,512]{2,1,0:T(8,128)(2,1)}), bf16[16,16,512]{2,1,0:T(8,128)(2,1)S(1)}, u32[]{:S(2)}, u32[]{:S(2)}) async-start(bf16[16,16,512]{2,1,0:T(8,128)(2,1)} %bitcast.6), calls=%async_computation.2 | async-start | bytes 524288 | tf_op jit(solution)/shard_map/all_to_all | solution.py:330
  158.1 1.2 collective-permute-start.30
  159.3 6.5 %collective-permute-start.31 = (f32[48,128]{1,0:T(8,128)S(1)}, f32[48,128]{1,0:T(8,128)S(1)}, u32[]{:S(2)}, u32[]{:S(2)}) collective-permute-start(f32[48,128]{1,0:T(8,128)S(1)} %add.7.s0), channel_id=1, source_target_pairs={{0,2},{1,3},{2,0},{3,1},{4,6},{5,7},{6,4},{7,5},{8,10},{9,11},{10,... | collective-permute-start | bytes 73736 | tf_op jit(solution)/shard_map/ppermute | solution.py:335
  159.8 7.8 %collective-permute-start.32 = (f32[48,128]{1,0:T(8,128)S(1)}, f32[48,128]{1,0:T(8,128)S(1)}, u32[]{:S(2)}, u32[]{:S(2)}) collective-permute-start(f32[48,128]{1,0:T(8,128)S(1)} %add.7.s0), channel_id=1, source_target_pairs={{0,4},{1,5},{2,6},{3,7},{4,0},{5,1},{6,2},{7,3},{8,12},{9,13},{10,... | collective-permute-start | bytes 73736 | tf_op jit(solution)/shard_map/ppermute | solution.py:335
  165.5 5.9 %collective-permute-start.33 = (f32[48,128]{1,0:T(8,128)S(1)}, f32[48,128]{1,0:T(8,128)S(1)}, u32[]{:S(2)}, u32[]{:S(2)}) collective-permute-start(f32[48,128]{1,0:T(8,128)S(1)} %add.7.s0), channel_id=1, source_target_pairs={{0,6},{1,7},{2,4},{3,5},{4,2},{5,3},{6,0},{7,1},{8,14},{9,15},{10,... | collective-permute-start | bytes 73736 | tf_op jit(solution)/shard_map/ppermute | solution.py:335
  172.2 14.7 %all-to-all-start.3 = ((bf16[16,96,128]{2,1,0:T(8,128)(2,1)}), bf16[16,96,128]{2,1,0:T(8,128)(2,1)S(1)}, u32[]{:S(2)}, u32[]{:S(2)}) async-start(bf16[16,96,128]{2,1,0:T(8,128)(2,1)} %get-tuple-element.42), calls=%async_computation.3 | async-start | bytes 786432 | tf_op jit(solution)/shard_map/all_to_all | solution.py:341

commit v2 on v1

--- a/solution.py
+++ b/solution.py
@@ -269,19 +269,19 @@
         both = jnp.concatenate([own[i], other[i]], axis=0)
         mixed = dot(high, both, TN) + dot(low, both, TN)
         value = (mixed - fock_rows(pieces, i, k, rows)) / gap[i : i + 1, :]
-        out[i] = value
+        out[:, i, :] = value
 
 
 def last_update(place, pieces, inverse, own, other, gap):
     r, k, n = own.shape
     vectors, coupling = pl.pallas_call(
         last_kernel,
-        out_shape=(array((r, k, n), F32), array((k, 2 * k), F32)),
+        out_shape=(array((k, r, n), F32), array((k, 2 * k), F32)),
         in_specs=[SMEM] + [VMEM] * 5,
         out_specs=(VMEM, VMEM),
         compiler_params=PARAMS,
     )(place, pieces, inverse, own, other, gap)
-    return jnp.transpose(vectors, (1, 0, 2)), coupling.T
+    return vectors, coupling.T
 
 
 def ring(step):

time: 191 us -> 190 us (level)
    unnamed x17 -> x16, local copies, waits for them, and re-layouts: 6.93 us -> 5.83 us
where the time goes in v2:
time: 190 us; the launch traced here: 189 us
  starting transfers between devices  84.7 us (45%)
  waiting for transfers between devices  62.6 us (33%)
  Pallas kernels  35.3 us (19%)
  local copies, waits for them, and re-layouts  5.83 us (3%)
    ppermute x2, waiting for transfers between devices, per_device(): far = lax.ppermute(add(mine_far, theirs_far, 0), 'gz', AHEAD)  18.4 us
    pallas_call x2, Pallas kernels, inverse_of(): pl.pallas_call(inverse_kernel, out_shape=keep((size, size), F32), in_spec...  16.2 us
    all_to_all x2, starting transfers between devices, per_device(): lax.all_to_all(fock.reshape(16, -1, fock.shape[1]), 'gy', 0, 0, tiled=True)  14.5 us
    all_to_all x2, starting transfers between devices, per_device(): pieces = lax.all_to_all(pieces, 'gy', 0, 0, tiled=True)  14.5 us
    ppermute x6, starting transfers between devices, per_device(): lax.ppermute(sums, 'gz', [(i, i ^ flip) for i in range(8)])  13 us
    ppermute x2, waiting for transfers between devices, per_device(): second = lax.ppermute(first, 'gz', AHEAD)  11.2 us
    ppermute x2, starting transfers between devices, per_device(): second = lax.ppermute(first, 'gz', AHEAD)  9.43 us
    ppermute x6, waiting for transfers between devices, per_device(): lax.ppermute(sums, 'gz', [(i, i ^ flip) for i in range(8)])  9.21 us
  transfers between devices with their start and end apart: 38, of which 17 were waited for; matrix products, arithmetic and copies ran while one was open for 0% of the time, Pallas kernels for 11%

profile of v2, /device:TPU:2, one launch (start us, length us, event | category | flops | bytes accessed | tf_op | source)
XLA Modules:
  0.0 189.4 jit_solution(8955566368848295621)
XLA Ops:
  0.6 1.3 copy.12
  2.0 3.0 %copy.11 = bf16[384,8,512]{2,0,1:T(8,128)(2,1)S(1)} copy(bf16[384,8,512]{2,1,0:T(8,128)(2,1)} %param.3) | data formatting | bytes 6291456 | tf_op args[0]
  5.1 1.7 shard_map.50
  6.8 0.1 collective-permute-start
  6.9 1.6 shard_map.52
  8.5 0.6 collective-permute-start.2
  9.1 1.1 collective-permute-done.2.theirs
  10.2 6.4 %collective-permute-start.3 = (bf16[256,384]{1,0:T(8,128)(2,1)S(1)}, bf16[256,384]{1,0:T(8,128)(2,1)S(1)}, u32[]{:S(2)}, u32[]{:S(2)}) collective-permute-start(bf16[256,384]{1,0:T(8,128)(2,1)S(1)} %shard_map.53), channel_id=1, source_target_pairs={{0,6},{1,3},{2,0},{3,5},{4,2},{5,7},{6,4},{7,1},{8,14},{9,11},{10,... | collective-permute-start | bytes 589832 | tf_op jit(solution)/shard_map/ppermute | solution.py:316
  16.7 9.0 %collective-permute-done.3.refs_0_ = bf16[256,384]{1,0:T(8,128)(2,1)S(1)} collective-permute-done((bf16[256,384]{1,0:T(8,128)(2,1)S(1)}, bf16[256,384]{1,0:T(8,128)(2,1)S(1)}, u32[]{:S(2)}, u32[]{:S(2)}) %collective-permute-start.3) | collective-permute-done | bytes 196640 | tf_op jit(solution)/shard_map/ppermute | solution.py:316
  25.8 4.6 %collective-permute-start.4 = (bf16[256,384]{1,0:T(8,128)(2,1)S(1)}, bf16[256,384]{1,0:T(8,128)(2,1)S(1)}, u32[]{:S(2)}, u32[]{:S(2)}) collective-permute-start(bf16[256,384]{1,0:T(8,128)(2,1)S(1)} %shard_map.54), channel_id=1, source_target_pairs={{0,6},{1,3},{2,0},{3,5},{4,2},{5,7},{6,4},{7,1},{8,14},{9,11},{10,... | collective-permute-start | bytes 589832 | tf_op jit(solution)/shard_map/ppermute | solution.py:319
  30.4 4.9 %collective-permute-done.4.refs_1_ = bf16[256,384]{1,0:T(8,128)(2,1)S(1)} collective-permute-done((bf16[256,384]{1,0:T(8,128)(2,1)S(1)}, bf16[256,384]{1,0:T(8,128)(2,1)S(1)}, u32[]{:S(2)}, u32[]{:S(2)}) %collective-permute-start.4) | collective-permute-done | bytes 196640 | tf_op jit(solution)/shard_map/ppermute | solution.py:319
  35.3 0.1 shard_map.55.refs_0_
  35.4 4.7 %collective-permute-start.5 = (bf16[256,384]{1,0:T(8,128)(2,1)S(1)}, bf16[256,384]{1,0:T(8,128)(2,1)S(1)}, u32[]{:S(2)}, u32[]{:S(2)}) collective-permute-start(bf16[256,384]{1,0:T(8,128)(2,1)S(1)} %shard_map.55.refs_0_), channel_id=1, source_target_pairs={{0,6},{1,3},{2,0},{3,5},{4,2},{5,7},{6,4},{7,1},{8,14},{9,11},{10,... | collective-permute-start | bytes 589832 | tf_op jit(solution)/shard_map/ppermute | solution.py:321
  40.1 5.1 %collective-permute-done.5.refs_1_ = bf16[256,384]{1,0:T(8,128)(2,1)S(1)} collective-permute-done((bf16[256,384]{1,0:T(8,128)(2,1)S(1)}, bf16[256,384]{1,0:T(8,128)(2,1)S(1)}, u32[]{:S(2)}, u32[]{:S(2)}) %collective-permute-start.5) | collective-permute-done | bytes 196640 | tf_op jit(solution)/shard_map/ppermute | solution.py:321
  45.2 2.8 %collective-permute-start.7 = (bf16[256,384]{1,0:T(8,128)(2,1)S(1)}, bf16[256,384]{1,0:T(8,128)(2,1)S(1)}, u32[]{:S(2)}, u32[]{:S(2)}) collective-permute-start(bf16[256,384]{1,0:T(8,128)(2,1)S(1)} %collective-permute-done.5.refs_1_), channel_id=1, source_target_pairs={{0,6},{1,3},{2,0},{3,5},{4,2},{5,7},{6,4},{7,1},{8,14},{9,11},{10,... | collective-permute-start | bytes 589832 | tf_op jit(solution)/shard_map/ppermute | solution.py:324
  48.0 5.2 %collective-permute-start.12 = (bf16[8,32,512]{2,1,0:T(8,128)(2,1)S(1)}, bf16[8,32,512]{2,1,0:T(8,128)(2,1)S(1)}, u32[]{:S(2)}, u32[]{:S(2)}) collective-permute-start(bf16[8,32,512]{2,1,0:T(8,128)(2,1)S(1)} %bitcast.20), channel_id=1, source_target_pairs={{0,128},{128,0},{1,129},{129,1},{2,130},{130,2},{3,131},{131,3},{4... | collective-permute-start | bytes 786440 | tf_op jit(solution)/shard_map/ppermute | solution.py:325
  53.3 0.5 collective-permute-start.9
  53.8 0.5 collective-permute-start.11
  54.3 5.4 %collective-permute-done.12.other.refs_10_ = bf16[8,32,512]{2,1,0:T(8,128)(2,1)S(1)} collective-permute-done((bf16[8,32,512]{2,1,0:T(8,128)(2,1)S(1)}, bf16[8,32,512]{2,1,0:T(8,128)(2,1)S(1)}, u32[]{:S(2)}, u32[]{:S(2)}) %collective-permute-start.12) | collective-permute-done | bytes 262176 | tf_op jit(solution)/shard_map/ppermute | solution.py:325
  59.7 0.6 shard_map.56.refs_11_
  60.4 2.3 %shard_map.57 = (bf16[256,512]{1,0:T(8,128)(2,1)S(1)}, f32[48,128]{1,0:T(8,128)S(1)}) custom-call(s32[3]{0:T(128)S(1)} %pad_add_fusion.refs_0_.place, bf16[256,384]{1,0:T(8,128)(2,1)S(1)} %shard_map.55.refs_0_, bf16[256,384]{1,0:T(8,128)(2,1)S(1)} %collective-permute-done.5.refs_1_, bf16[256,384]{1,0:T(8,128)(2,1)S(1)} %collective-permute-done.6.refs_2_, ...), custom_call_target="tpu_custom_call" | custom-call | tf_op jit(solution)/shard_map/pallas_call | solution.py:155
  62.7 0.7 copy-done.6
  63.4 7.3 %all-to-all-start = ((bf16[16,16,512]{2,1,0:T(8,128)(2,1)}), bf16[16,16,512]{2,1,0:T(8,128)(2,1)S(1)}, u32[]{:S(2)}, u32[]{:S(2)}) async-start(bf16[16,16,512]{2,1,0:T(8,128)(2,1)} %bitcast.24), calls=%async_computation | async-start | bytes 524288 | tf_op jit(solution)/shard_map/all_to_all | solution.py:330
  70.7 1.2 collective-permute-done.13
  71.9 1.1 collective-permute-start.14
  73.0 3.0 %collective-permute-start.15 = (f32[48,128]{1,0:T(8,128)S(1)}, f32[48,128]{1,0:T(8,128)S(1)}, u32[]{:S(2)}, u32[]{:S(2)}) collective-permute-start(f32[48,128]{1,0:T(8,128)S(1)} %add.6.s0), channel_id=1, source_target_pairs={{0,4},{1,5},{2,6},{3,7},{4,0},{5,1},{6,2},{7,3},{8,12},{9,13},{10,... | collective-permute-start | bytes 73736 | tf_op jit(solution)/shard_map/ppermute | solution.py:335
  76.0 2.4 %collective-permute-start.16 = (f32[48,128]{1,0:T(8,128)S(1)}, f32[48,128]{1,0:T(8,128)S(1)}, u32[]{:S(2)}, u32[]{:S(2)}) collective-permute-start(f32[48,128]{1,0:T(8,128)S(1)} %add.6.s0), channel_id=1, source_target_pairs={{0,6},{1,7},{2,4},{3,5},{4,2},{5,3},{6,0},{7,1},{8,14},{9,15},{10,... | collective-permute-start | bytes 73736 | tf_op jit(solution)/shard_map/ppermute | solution.py:335
  78.4 2.5 %collective-permute-done.15.s2 = f32[48,128]{1,0:T(8,128)S(1)} collective-permute-done((f32[48,128]{1,0:T(8,128)S(1)}, f32[48,128]{1,0:T(8,128)S(1)}, u32[]{:S(2)}, u32[]{:S(2)}) %collective-permute-start.15) | collective-permute-done | bytes 24608 | tf_op jit(solution)/shard_map/ppermute | solution.py:335
  80.9 1.1 collective-permute-done.16.s3
  82.0 0.6 shard_map.58
  82.6 0.7 copy-done.4
  83.3 7.2 %all-to-all-start.1 = ((bf16[16,96,128]{2,1,0:T(8,128)(2,1)}), bf16[16,96,128]{2,1,0:T(8,128)(2,1)}, u32[]{:S(2)}, u32[]{:S(2)}) async-start(bf16[16,96,128]{2,1,0:T(8,128)(2,1)} %copy-done.4), calls=%async_computation.1 | async-start | bytes 786432 | tf_op jit(solution)/shard_map/all_to_all | solution.py:341
  90.6 8.8 %shard_map.59.inverse = f32[64,64]{1,0:T(8,128)} custom-call(f32[32,128]{1,0:T(8,128)} %get-tuple-element.33.totals), custom_call_target="tpu_custom_call" | custom-call | tf_op jit(solution)/shard_map/pallas_call | solution.py:214
  99.3 1.8 shard_map.60.refs_1_.own.refs_9_
  101.1 1.7 shard_map.61
  102.8 0.1 collective-permute-start.17
  102.9 1.6 shard_map.63
  104.5 0.6 collective-permute-start.19
  105.1 1.1 collective-permute-done.19.theirs
  106.2 2.5 %collective-permute-start.20 = (bf16[256,384]{1,0:T(8,128)(2,1)S(1)}, bf16[256,384]{1,0:T(8,128)(2,1)S(1)}, u32[]{:S(2)}, u32[]{:S(2)}) collective-permute-start(bf16[256,384]{1,0:T(8,128)(2,1)S(1)} %shard_map.64), channel_id=1, source_target_pairs={{0,6},{1,3},{2,0},{3,5},{4,2},{5,7},{6,4},{7,1},{8,14},{9,11},{10,... | collective-permute-start | bytes 589832 | tf_op jit(solution)/shard_map/ppermute | solution.py:316
  108.7 0.6 collective-permute-start.18
  109.4 9.5 %collective-permute-done.20.refs_0_ = bf16[256,384]{1,0:T(8,128)(2,1)S(1)} collective-permute-done((bf16[256,384]{1,0:T(8,128)(2,1)S(1)}, bf16[256,384]{1,0:T(8,128)(2,1)S(1)}, u32[]{:S(2)}, u32[]{:S(2)}) %collective-permute-start.20) | collective-permute-done | bytes 196640 | tf_op jit(solution)/shard_map/ppermute | solution.py:316
  118.9 3.4 %collective-permute-start.21 = (bf16[256,384]{1,0:T(8,128)(2,1)S(1)}, bf16[256,384]{1,0:T(8,128)(2,1)S(1)}, u32[]{:S(2)}, u32[]{:S(2)}) collective-permute-start(bf16[256,384]{1,0:T(8,128)(2,1)S(1)} %shard_map.65), channel_id=1, source_target_pairs={{0,6},{1,3},{2,0},{3,5},{4,2},{5,7},{6,4},{7,1},{8,14},{9,11},{10,... | collective-permute-start | bytes 589832 | tf_op jit(solution)/shard_map/ppermute | solution.py:319
  122.3 3.3 %collective-permute-done.21.refs_1_ = bf16[256,384]{1,0:T(8,128)(2,1)S(1)} collective-permute-done((bf16[256,384]{1,0:T(8,128)(2,1)S(1)}, bf16[256,384]{1,0:T(8,128)(2,1)S(1)}, u32[]{:S(2)}, u32[]{:S(2)}) %collective-permute-start.21) | collective-permute-done | bytes 196640 | tf_op jit(solution)/shard_map/ppermute | solution.py:319
  125.6 4.7 %collective-permute-start.22 = (bf16[256,384]{1,0:T(8,128)(2,1)S(1)}, bf16[256,384]{1,0:T(8,128)(2,1)S(1)}, u32[]{:S(2)}, u32[]{:S(2)}) collective-permute-start(bf16[256,384]{1,0:T(8,128)(2,1)S(1)} %shard_map.66.refs_0_), channel_id=1, source_target_pairs={{0,6},{1,3},{2,0},{3,5},{4,2},{5,7},{6,4},{7,1},{8,14},{9,11},{10,... | collective-permute-start | bytes 589832 | tf_op jit(solution)/shard_map/ppermute | solution.py:321
  130.3 6.2 %collective-permute-done.22.refs_1_ = bf16[256,384]{1,0:T(8,128)(2,1)S(1)} collective-permute-done((bf16[256,384]{1,0:T(8,128)(2,1)S(1)}, bf16[256,384]{1,0:T(8,128)(2,1)S(1)}, u32[]{:S(2)}, u32[]{:S(2)}) %collective-permute-start.22) | collective-permute-done | bytes 196640 | tf_op jit(solution)/shard_map/ppermute | solution.py:321
  136.5 2.4 %collective-permute-start.24 = (bf16[256,384]{1,0:T(8,128)(2,1)S(1)}, bf16[256,384]{1,0:T(8,128)(2,1)S(1)}, u32[]{:S(2)}, u32[]{:S(2)}) collective-permute-start(bf16[256,384]{1,0:T(8,128)(2,1)S(1)} %collective-permute-done.22.refs_1_), channel_id=1, source_target_pairs={{0,6},{1,3},{2,0},{3,5},{4,2},{5,7},{6,4},{7,1},{8,14},{9,11},{10,... | collective-permute-start | bytes 589832 | tf_op jit(solution)/shard_map/ppermute | solution.py:324
  138.9 0.5 collective-permute-start.26
  139.4 3.7 %collective-permute-done.24.refs_3_ = bf16[256,384]{1,0:T(8,128)(2,1)S(1)} collective-permute-done((bf16[256,384]{1,0:T(8,128)(2,1)S(1)}, bf16[256,384]{1,0:T(8,128)(2,1)S(1)}, u32[]{:S(2)}, u32[]{:S(2)}) %collective-permute-start.24) | collective-permute-done | bytes 196640 | tf_op jit(solution)/shard_map/ppermute | solution.py:324
  143.2 2.4 %collective-permute-start.28 = (bf16[256,384]{1,0:T(8,128)(2,1)S(1)}, bf16[256,384]{1,0:T(8,128)(2,1)S(1)}, u32[]{:S(2)}, u32[]{:S(2)}) collective-permute-start(bf16[256,384]{1,0:T(8,128)(2,1)S(1)} %collective-permute-done.24.refs_3_), channel_id=1, source_target_pairs={{0,1},{1,0},{2,3},{3,2},{4,5},{5,4},{6,7},{7,6},{8,9},{9,8},{10,11... | collective-permute-start | bytes 589832 | tf_op jit(solution)/shard_map/ppermute | solution.py:327
  145.6 1.8 collective-permute-done.29.other.refs_10_
  147.4 0.6 shard_map.67.refs_11_
  148.1 2.7 %shard_map.68 = (bf16[256,512]{1,0:T(8,128)(2,1)}, f32[48,128]{1,0:T(8,128)S(1)}) custom-call(s32[3]{0:T(128)S(1)} %pad_add_fusion.refs_0_.place, bf16[256,384]{1,0:T(8,128)(2,1)S(1)} %shard_map.66.refs_0_, bf16[256,384]{1,0:T(8,128)(2,1)S(1)} %collective-permute-done.22.refs_1_, bf16[256,384]{1,0:T(8,128)(2,1)S(1)} %collective-permute-done.23.refs_2_, ...), custom_call_target="tpu_custom_call" | custom-call | tf_op jit(solution)/shard_map/pallas_call | solution.py:155
  150.8 7.2 %all-to-all-start.2 = ((bf16[16,16,512]{2,1,0:T(8,128)(2,1)}), bf16[16,16,512]{2,1,0:T(8,128)(2,1)S(1)}, u32[]{:S(2)}, u32[]{:S(2)}) async-start(bf16[16,16,512]{2,1,0:T(8,128)(2,1)} %bitcast.6), calls=%async_computation.2 | async-start | bytes 524288 | tf_op jit(solution)/shard_map/all_to_all | solution.py:330
  158.1 1.2 collective-permute-done.30
  159.3 0.5 collective-permute-start.31
  159.8 5.7 %collective-permute-start.32 = (f32[48,128]{1,0:T(8,128)S(1)}, f32[48,128]{1,0:T(8,128)S(1)}, u32[]{:S(2)}, u32[]{:S(2)}) collective-permute-start(f32[48,128]{1,0:T(8,128)S(1)} %add.7.s0), channel_id=1, source_target_pairs={{0,4},{1,5},{2,6},{3,7},{4,0},{5,1},{6,2},{7,3},{8,12},{9,13},{10,... | collective-permute-start | bytes 73736 | tf_op jit(solution)/shard_map/ppermute | solution.py:335
  165.5 0.3 collective-permute-start.33
  165.8 1.8 collective-permute-done.32.s2
  167.6 3.9 %collective-permute-done.33.s3 = f32[48,128]{1,0:T(8,128)S(1)} collective-permute-done((f32[48,128]{1,0:T(8,128)S(1)}, f32[48,128]{1,0:T(8,128)S(1)}, u32[]{:S(2)}, u32[]{:S(2)}) %collective-permute-start.33) | collective-permute-done | bytes 24608 | tf_op jit(solution)/shard_map/ppermute | solution.py:335
  171.4 0.8 shard_map.69
  172.2 7.2 %all-to-all-start.3 = ((bf16[16,96,128]{2,1,0:T(8,128)(2,1)}), bf16[16,96,128]{2,1,0:T(8,128)(2,1)S(1)}, u32[]{:S(2)}, u32[]{:S(2)}) async-start(bf16[16,96,128]{2,1,0:T(8,128)(2,1)} %get-tuple-element.42), calls=%async_computation.3 | async-start | bytes 786432 | tf_op jit(solution)/shard_map/all_to_all | solution.py:341
  179.5 7.4 %shard_map.70.inverse = f32[64,64]{1,0:T(8,128)S(1)} custom-call(f32[32,128]{1,0:T(8,128)S(1)} %get-tuple-element.43.totals), custom_call_target="tpu_custom_call" | custom-call | tf_op jit(solution)/shard_map/pallas_call | solution.py:214
  186.9 2.5 %shard_map.71 = (f32[32,8,512]{2,1,0:T(8,128)}, f32[32,64]{1,0:T(8,128)}) custom-call(s32[3]{0:T(128)S(1)} %pad_add_fusion.refs_0_.place, bf16[16,96,128]{2,1,0:T(8,128)(2,1)S(1)} %all-to-all-done.3.pieces, f32[64,64]{1,0:T(8,128)S(1)} %shard_map.70.inverse, bf16[8,32,512]{2,1,0:T(8,128)(2,1)} %copy-done, bf16[8,32,512]{2,1,0:T(8,128)(2,1)} %copy-done.2, ...), custom_call_target="tpu_custom_call" | custom-call | tf_op jit(solution)/shard_map/pallas_call | solution.py:277
  (53 shorter events, 0.6 us)
Async XLA Ops:
  2.0 58.4 %copy-start.1 = (bf16[32,8,512]{2,0,1:T(8,128)(2,1)}, bf16[32,8,512]{2,0,1:T(8,128)(2,1)S(1)}, u32[]{:S(2)}) copy-start(bf16[32,8,512]{2,0,1:T(8,128)(2,1)S(1)} %copy.12) | copy-start | bytes 786436
  6.8 9.8 %collective-permute-start = (bf16[3,256,384]{2,1,0:T(8,128)(2,1)S(1)}, bf16[3,256,384]{2,1,0:T(8,128)(2,1)S(1)}, u32[]{:S(2)}, u32[]{:S(2)}) collective-permute-start(bf16[3,256,384]{2,1,0:T(8,128)(2,1)S(1)} %get-tuple-element.25), channel_id=1, source_target_pairs={{0,1},{1,0},{2,3},{3,2},{4,5},{5,4},{6,7},{7,6},{8,9},{9,8},{10,11... | collective-permute-start | bytes 1769480 | tf_op jit(solution)/shard_map/ppermute | solution.py:317
  8.5 51.2 %copy-start.5 = (f32[8,512]{1,0:T(8,128)S(1)}, f32[8,512]{1,0:T(8,128)}, u32[]{:S(2)}) copy-start(f32[8,512]{1,0:T(8,128)} %gap.7) | copy-start | bytes 49156
  8.5 1.7 collective-permute-start.2
  10.2 15.5 %collective-permute-start.3 = (bf16[256,384]{1,0:T(8,128)(2,1)S(1)}, bf16[256,384]{1,0:T(8,128)(2,1)S(1)}, u32[]{:S(2)}, u32[]{:S(2)}) collective-permute-start(bf16[256,384]{1,0:T(8,128)(2,1)S(1)} %shard_map.53), channel_id=1, source_target_pairs={{0,6},{1,3},{2,0},{3,5},{4,2},{5,7},{6,4},{7,1},{8,14},{9,11},{10,... | collective-permute-start | bytes 589832 | tf_op jit(solution)/shard_map/ppermute | solution.py:316
  16.6 13.8 %collective-permute-start.1 = (bf16[256,384]{1,0:T(8,128)(2,1)S(1)}, bf16[256,384]{1,0:T(8,128)(2,1)S(1)}, u32[]{:S(2)}, u32[]{:S(2)}) collective-permute-start(bf16[256,384]{1,0:T(8,128)(2,1)S(1)} %shard_map.51), channel_id=1, source_target_pairs={{0,2},{1,7},{2,4},{3,1},{4,6},{5,3},{6,0},{7,5},{8,10},{9,15},{10,... | collective-permute-start | bytes 589832 | tf_op jit(solution)/shard_map/ppermute | solution.py:318
  25.8 9.6 %collective-permute-start.4 = (bf16[256,384]{1,0:T(8,128)(2,1)S(1)}, bf16[256,384]{1,0:T(8,128)(2,1)S(1)}, u32[]{:S(2)}, u32[]{:S(2)}) collective-permute-start(bf16[256,384]{1,0:T(8,128)(2,1)S(1)} %shard_map.54), channel_id=1, source_target_pairs={{0,6},{1,3},{2,0},{3,5},{4,2},{5,7},{6,4},{7,1},{8,14},{9,11},{10,... | collective-permute-start | bytes 589832 | tf_op jit(solution)/shard_map/ppermute | solution.py:319
  35.4 9.8 %collective-permute-start.5 = (bf16[256,384]{1,0:T(8,128)(2,1)S(1)}, bf16[256,384]{1,0:T(8,128)(2,1)S(1)}, u32[]{:S(2)}, u32[]{:S(2)}) collective-permute-start(bf16[256,384]{1,0:T(8,128)(2,1)S(1)} %shard_map.55.refs_0_), channel_id=1, source_target_pairs={{0,6},{1,3},{2,0},{3,5},{4,2},{5,7},{6,4},{7,1},{8,14},{9,11},{10,... | collective-permute-start | bytes 589832 | tf_op jit(solution)/shard_map/ppermute | solution.py:321
  40.1 13.6 %collective-permute-start.6 = (bf16[256,384]{1,0:T(8,128)(2,1)S(1)}, bf16[256,384]{1,0:T(8,128)(2,1)S(1)}, u32[]{:S(2)}, u32[]{:S(2)}) collective-permute-start(bf16[256,384]{1,0:T(8,128)(2,1)S(1)} %shard_map.55.refs_0_), channel_id=1, source_target_pairs={{0,2},{1,7},{2,4},{3,1},{4,6},{5,3},{6,0},{7,5},{8,10},{9,15},{10,... | collective-permute-start | bytes 589832 | tf_op jit(solution)/shard_map/ppermute | solution.py:323
  45.2 8.6 %collective-permute-start.7 = (bf16[256,384]{1,0:T(8,128)(2,1)S(1)}, bf16[256,384]{1,0:T(8,128)(2,1)S(1)}, u32[]{:S(2)}, u32[]{:S(2)}) collective-permute-start(bf16[256,384]{1,0:T(8,128)(2,1)S(1)} %collective-permute-done.5.refs_1_), channel_id=1, source_target_pairs={{0,6},{1,3},{2,0},{3,5},{4,2},{5,7},{6,4},{7,1},{8,14},{9,11},{10,... | collective-permute-start | bytes 589832 | tf_op jit(solution)/shard_map/ppermute | solution.py:324
  48.0 11.7 %collective-permute-start.12 = (bf16[8,32,512]{2,1,0:T(8,128)(2,1)S(1)}, bf16[8,32,512]{2,1,0:T(8,128)(2,1)S(1)}, u32[]{:S(2)}, u32[]{:S(2)}) collective-permute-start(bf16[8,32,512]{2,1,0:T(8,128)(2,1)S(1)} %bitcast.20), channel_id=1, source_target_pairs={{0,128},{128,0},{1,129},{129,1},{2,130},{130,2},{3,131},{131,3},{4... | collective-permute-start | bytes 786440 | tf_op jit(solution)/shard_map/ppermute | solution.py:325
  53.3 7.1 %collective-permute-start.8 = (bf16[256,384]{1,0:T(8,128)(2,1)S(1)}, bf16[256,384]{1,0:T(8,128)(2,1)S(1)}, u32[]{:S(2)}, u32[]{:S(2)}) collective-permute-start(bf16[256,384]{1,0:T(8,128)(2,1)S(1)} %shard_map.55.refs_0_), channel_id=1, source_target_pairs={{0,1},{1,0},{2,3},{3,2},{4,5},{5,4},{6,7},{7,6},{8,9},{9,8},{10,11... | collective-permute-start | bytes 589832 | tf_op jit(solution)/shard_map/ppermute | solution.py:322
  53.3 7.1 %collective-permute-start.9 = (bf16[256,384]{1,0:T(8,128)(2,1)S(1)}, bf16[256,384]{1,0:T(8,128)(2,1)S(1)}, u32[]{:S(2)}, u32[]{:S(2)}) collective-permute-start(bf16[256,384]{1,0:T(8,128)(2,1)S(1)} %collective-permute-done.5.refs_1_), channel_id=1, source_target_pairs={{0,1},{1,0},{2,3},{3,2},{4,5},{5,4},{6,7},{7,6},{8,9},{9,8},{10,11... | collective-permute-start | bytes 589832 | tf_op jit(solution)/shard_map/ppermute | solution.py:327
  53.8 6.6 %collective-permute-start.10 = (bf16[256,384]{1,0:T(8,128)(2,1)S(1)}, bf16[256,384]{1,0:T(8,128)(2,1)S(1)}, u32[]{:S(2)}, u32[]{:S(2)}) collective-permute-start(bf16[256,384]{1,0:T(8,128)(2,1)S(1)} %collective-permute-done.6.refs_2_), channel_id=1, source_target_pairs={{0,1},{1,0},{2,3},{3,2},{4,5},{5,4},{6,7},{7,6},{8,9},{9,8},{10,11... | collective-permute-start | bytes 589832 | tf_op jit(solution)/shard_map/ppermute | solution.py:327
  53.8 6.6 %collective-permute-start.11 = (bf16[256,384]{1,0:T(8,128)(2,1)S(1)}, bf16[256,384]{1,0:T(8,128)(2,1)S(1)}, u32[]{:S(2)}, u32[]{:S(2)}) collective-permute-start(bf16[256,384]{1,0:T(8,128)(2,1)S(1)} %collective-permute-done.7.refs_3_), channel_id=1, source_target_pairs={{0,1},{1,0},{2,3},{3,2},{4,5},{5,4},{6,7},{7,6},{8,9},{9,8},{10,11... | collective-permute-start | bytes 589832 | tf_op jit(solution)/shard_map/ppermute | solution.py:327
  59.7 3.0 %copy-start.3 = (bf16[8,32,512]{2,1,0:T(8,128)(2,1)}, bf16[8,32,512]{2,1,0:T(8,128)(2,1)S(1)}, u32[]{:S(2)}) copy-start(bf16[8,32,512]{2,1,0:T(8,128)(2,1)S(1)} %collective-permute-done.12.other.refs_10_) | copy-start | bytes 786436
  62.7 0.7 copy-start.6
  63.4 18.5 %all-to-all-start = ((bf16[16,16,512]{2,1,0:T(8,128)(2,1)}), bf16[16,16,512]{2,1,0:T(8,128)(2,1)S(1)}, u32[]{:S(2)}, u32[]{:S(2)}) async-start(bf16[16,16,512]{2,1,0:T(8,128)(2,1)} %bitcast.24), calls=%async_computation | async-start | bytes 524288 | tf_op jit(solution)/shard_map/all_to_all | solution.py:330
  70.7 1.2 collective-permute-start.13
  71.9 6.5 %collective-permute-start.14 = (f32[48,128]{1,0:T(8,128)S(1)}, f32[48,128]{1,0:T(8,128)S(1)}, u32[]{:S(2)}, u32[]{:S(2)}) collective-permute-start(f32[48,128]{1,0:T(8,128)S(1)} %add.6.s0), channel_id=1, source_target_pairs={{0,2},{1,3},{2,0},{3,1},{4,6},{5,7},{6,4},{7,5},{8,10},{9,11},{10,... | collective-permute-start | bytes 73736 | tf_op jit(solution)/shard_map/ppermute | solution.py:335
  73.0 7.9 %collective-permute-start.15 = (f32[48,128]{1,0:T(8,128)S(1)}, f32[48,128]{1,0:T(8,128)S(1)}, u32[]{:S(2)}, u32[]{:S(2)}) collective-permute-start(f32[48,128]{1,0:T(8,128)S(1)} %add.6.s0), channel_id=1, source_target_pairs={{0,4},{1,5},{2,6},{3,7},{4,0},{5,1},{6,2},{7,3},{8,12},{9,13},{10,... | collective-permute-start | bytes 73736 | tf_op jit(solution)/shard_map/ppermute | solution.py:335
  76.0 5.9 %collective-permute-start.16 = (f32[48,128]{1,0:T(8,128)S(1)}, f32[48,128]{1,0:T(8,128)S(1)}, u32[]{:S(2)}, u32[]{:S(2)}) collective-permute-start(f32[48,128]{1,0:T(8,128)S(1)} %add.6.s0), channel_id=1, source_target_pairs={{0,6},{1,7},{2,4},{3,5},{4,2},{5,3},{6,0},{7,1},{8,14},{9,15},{10,... | collective-permute-start | bytes 73736 | tf_op jit(solution)/shard_map/ppermute | solution.py:335
  82.6 0.7 copy-start.4
  83.3 16.0 %all-to-all-start.1 = ((bf16[16,96,128]{2,1,0:T(8,128)(2,1)}), bf16[16,96,128]{2,1,0:T(8,128)(2,1)}, u32[]{:S(2)}, u32[]{:S(2)}) async-start(bf16[16,96,128]{2,1,0:T(8,128)(2,1)} %copy-done.4), calls=%async_computation.1 | async-start | bytes 786432 | tf_op jit(solution)/shard_map/all_to_all | solution.py:341
  101.1 47.0 %copy-start = (bf16[8,32,512]{2,1,0:T(8,128)(2,1)}, bf16[8,32,512]{2,1,0:T(8,128)(2,1)S(1)}, u32[]{:S(2)}) copy-start(bf16[8,32,512]{2,1,0:T(8,128)(2,1)S(1)} %shard_map.60.refs_1_.own.refs_9_) | copy-start | bytes 786436
  102.8 5.9 %collective-permute-start.17 = (bf16[3,256,384]{2,1,0:T(8,128)(2,1)S(1)}, bf16[3,256,384]{2,1,0:T(8,128)(2,1)S(1)}, u32[]{:S(2)}, u32[]{:S(2)}) collective-permute-start(bf16[3,256,384]{2,1,0:T(8,128)(2,1)S(1)} %get-tuple-element.35), channel_id=1, source_target_pairs={{0,1},{1,0},{2,3},{3,2},{4,5},{5,4},{6,7},{7,6},{8,9},{9,8},{10,11... | collective-permute-start | bytes 1769480 | tf_op jit(solution)/shard_map/ppermute | solution.py:317
  104.5 1.7 collective-permute-start.19
  106.2 12.6 %collective-permute-start.20 = (bf16[256,384]{1,0:T(8,128)(2,1)S(1)}, bf16[256,384]{1,0:T(8,128)(2,1)S(1)}, u32[]{:S(2)}, u32[]{:S(2)}) collective-permute-start(bf16[256,384]{1,0:T(8,128)(2,1)S(1)} %shard_map.64), channel_id=1, source_target_pairs={{0,6},{1,3},{2,0},{3,5},{4,2},{5,7},{6,4},{7,1},{8,14},{9,11},{10,... | collective-permute-start | bytes 589832 | tf_op jit(solution)/shard_map/ppermute | solution.py:316
  108.7 13.6 %collective-permute-start.18 = (bf16[256,384]{1,0:T(8,128)(2,1)S(1)}, bf16[256,384]{1,0:T(8,128)(2,1)S(1)}, u32[]{:S(2)}, u32[]{:S(2)}) collective-permute-start(bf16[256,384]{1,0:T(8,128)(2,1)S(1)} %shard_map.62), channel_id=1, source_target_pairs={{0,2},{1,7},{2,4},{3,1},{4,6},{5,3},{6,0},{7,5},{8,10},{9,15},{10,... | collective-permute-start | bytes 589832 | tf_op jit(solution)/shard_map/ppermute | solution.py:318
  118.9 6.6 %collective-permute-start.21 = (bf16[256,384]{1,0:T(8,128)(2,1)S(1)}, bf16[256,384]{1,0:T(8,128)(2,1)S(1)}, u32[]{:S(2)}, u32[]{:S(2)}) collective-permute-start(bf16[256,384]{1,0:T(8,128)(2,1)S(1)} %shard_map.65), channel_id=1, source_target_pairs={{0,6},{1,3},{2,0},{3,5},{4,2},{5,7},{6,4},{7,1},{8,14},{9,11},{10,... | collective-permute-start | bytes 589832 | tf_op jit(solution)/shard_map/ppermute | solution.py:319
  125.6 10.9 %collective-permute-start.22 = (bf16[256,384]{1,0:T(8,128)(2,1)S(1)}, bf16[256,384]{1,0:T(8,128)(2,1)S(1)}, u32[]{:S(2)}, u32[]{:S(2)}) collective-permute-start(bf16[256,384]{1,0:T(8,128)(2,1)S(1)} %shard_map.66.refs_0_), channel_id=1, source_target_pairs={{0,6},{1,3},{2,0},{3,5},{4,2},{5,7},{6,4},{7,1},{8,14},{9,11},{10,... | collective-permute-start | bytes 589832 | tf_op jit(solution)/shard_map/ppermute | solution.py:321
  130.3 9.1 %collective-permute-start.23 = (bf16[256,384]{1,0:T(8,128)(2,1)S(1)}, bf16[256,384]{1,0:T(8,128)(2,1)S(1)}, u32[]{:S(2)}, u32[]{:S(2)}) collective-permute-start(bf16[256,384]{1,0:T(8,128)(2,1)S(1)} %shard_map.66.refs_0_), channel_id=1, source_target_pairs={{0,2},{1,7},{2,4},{3,1},{4,6},{5,3},{6,0},{7,5},{8,10},{9,15},{10,... | collective-permute-start | bytes 589832 | tf_op jit(solution)/shard_map/ppermute | solution.py:323
  136.5 6.7 %collective-permute-start.24 = (bf16[256,384]{1,0:T(8,128)(2,1)S(1)}, bf16[256,384]{1,0:T(8,128)(2,1)S(1)}, u32[]{:S(2)}, u32[]{:S(2)}) collective-permute-start(bf16[256,384]{1,0:T(8,128)(2,1)S(1)} %collective-permute-done.22.refs_1_), channel_id=1, source_target_pairs={{0,6},{1,3},{2,0},{3,5},{4,2},{5,7},{6,4},{7,1},{8,14},{9,11},{10,... | collective-permute-start | bytes 589832 | tf_op jit(solution)/shard_map/ppermute | solution.py:324
  138.9 8.5 %collective-permute-start.29 = (bf16[8,32,512]{2,1,0:T(8,128)(2,1)S(1)}, bf16[8,32,512]{2,1,0:T(8,128)(2,1)S(1)}, u32[]{:S(2)}, u32[]{:S(2)}) collective-permute-start(bf16[8,32,512]{2,1,0:T(8,128)(2,1)S(1)} %shard_map.60.refs_1_.own.refs_9_), channel_id=1, source_target_pairs={{0,128},{128,0},{1,129},{129,1},{2,130},{130,2},{3,131},{131,3},{4... | collective-permute-start | bytes 786440 | tf_op jit(solution)/shard_map/ppermute | solution.py:325
  138.9 9.1 %collective-permute-start.25 = (bf16[256,384]{1,0:T(8,128)(2,1)S(1)}, bf16[256,384]{1,0:T(8,128)(2,1)S(1)}, u32[]{:S(2)}, u32[]{:S(2)}) collective-permute-start(bf16[256,384]{1,0:T(8,128)(2,1)S(1)} %shard_map.66.refs_0_), channel_id=1, source_target_pairs={{0,1},{1,0},{2,3},{3,2},{4,5},{5,4},{6,7},{7,6},{8,9},{9,8},{10,11... | collective-permute-start | bytes 589832 | tf_op jit(solution)/shard_map/ppermute | solution.py:322
  138.9 9.1 %collective-permute-start.26 = (bf16[256,384]{1,0:T(8,128)(2,1)S(1)}, bf16[256,384]{1,0:T(8,128)(2,1)S(1)}, u32[]{:S(2)}, u32[]{:S(2)}) collective-permute-start(bf16[256,384]{1,0:T(8,128)(2,1)S(1)} %collective-permute-done.22.refs_1_), channel_id=1, source_target_pairs={{0,1},{1,0},{2,3},{3,2},{4,5},{5,4},{6,7},{7,6},{8,9},{9,8},{10,11... | collective-permute-start | bytes 589832 | tf_op jit(solution)/shard_map/ppermute | solution.py:327
  139.4 8.6 %collective-permute-start.27 = (bf16[256,384]{1,0:T(8,128)(2,1)S(1)}, bf16[256,384]{1,0:T(8,128)(2,1)S(1)}, u32[]{:S(2)}, u32[]{:S(2)}) collective-permute-start(bf16[256,384]{1,0:T(8,128)(2,1)S(1)} %collective-permute-done.23.refs_2_), channel_id=1, source_target_pairs={{0,1},{1,0},{2,3},{3,2},{4,5},{5,4},{6,7},{7,6},{8,9},{9,8},{10,11... | collective-permute-start | bytes 589832 | tf_op jit(solution)/shard_map/ppermute | solution.py:327
  143.2 4.9 %collective-permute-start.28 = (bf16[256,384]{1,0:T(8,128)(2,1)S(1)}, bf16[256,384]{1,0:T(8,128)(2,1)S(1)}, u32[]{:S(2)}, u32[]{:S(2)}) collective-permute-start(bf16[256,384]{1,0:T(8,128)(2,1)S(1)} %collective-permute-done.24.refs_3_), channel_id=1, source_target_pairs={{0,1},{1,0},{2,3},{3,2},{4,5},{5,4},{6,7},{7,6},{8,9},{9,8},{10,11... | collective-permute-start | bytes 589832 | tf_op jit(solution)/shard_map/ppermute | solution.py:327
  147.4 3.4 %copy-start.2 = (bf16[8,32,512]{2,1,0:T(8,128)(2,1)}, bf16[8,32,512]{2,1,0:T(8,128)(2,1)S(1)}, u32[]{:S(2)}) copy-start(bf16[8,32,512]{2,1,0:T(8,128)(2,1)S(1)} %collective-permute-done.29.other.refs_10_) | copy-start | bytes 786436
  150.8 20.6 %all-to-all-start.2 = ((bf16[16,16,512]{2,1,0:T(8,128)(2,1)}), bf16[16,16,512]{2,1,0:T(8,128)(2,1)S(1)}, u32[]{:S(2)}, u32[]{:S(2)}) async-start(bf16[16,16,512]{2,1,0:T(8,128)(2,1)} %bitcast.6), calls=%async_computation.2 | async-start | bytes 524288 | tf_op jit(solution)/shard_map/all_to_all | solution.py:330
  158.1 1.2 collective-permute-start.30
  159.3 6.5 %collective-permute-start.31 = (f32[48,128]{1,0:T(8,128)S(1)}, f32[48,128]{1,0:T(8,128)S(1)}, u32[]{:S(2)}, u32[]{:S(2)}) collective-permute-start(f32[48,128]{1,0:T(8,128)S(1)} %add.7.s0), channel_id=1, source_target_pairs={{0,2},{1,3},{2,0},{3,1},{4,6},{5,7},{6,4},{7,5},{8,10},{9,11},{10,... | collective-permute-start | bytes 73736 | tf_op jit(solution)/shard_map/ppermute | solution.py:335
  159.8 7.8 %collective-permute-start.32 = (f32[48,128]{1,0:T(8,128)S(1)}, f32[48,128]{1,0:T(8,128)S(1)}, u32[]{:S(2)}, u32[]{:S(2)}) collective-permute-start(f32[48,128]{1,0:T(8,128)S(1)} %add.7.s0), channel_id=1, source_target_pairs={{0,4},{1,5},{2,6},{3,7},{4,0},{5,1},{6,2},{7,3},{8,12},{9,13},{10,... | collective-permute-start | bytes 73736 | tf_op jit(solution)/shard_map/ppermute | solution.py:335
  165.5 5.9 %collective-permute-start.33 = (f32[48,128]{1,0:T(8,128)S(1)}, f32[48,128]{1,0:T(8,128)S(1)}, u32[]{:S(2)}, u32[]{:S(2)}) collective-permute-start(f32[48,128]{1,0:T(8,128)S(1)} %add.7.s0), channel_id=1, source_target_pairs={{0,6},{1,7},{2,4},{3,5},{4,2},{5,3},{6,0},{7,1},{8,14},{9,15},{10,... | collective-permute-start | bytes 73736 | tf_op jit(solution)/shard_map/ppermute | solution.py:335
  172.2 14.7 %all-to-all-start.3 = ((bf16[16,96,128]{2,1,0:T(8,128)(2,1)}), bf16[16,96,128]{2,1,0:T(8,128)(2,1)S(1)}, u32[]{:S(2)}, u32[]{:S(2)}) async-start(bf16[16,96,128]{2,1,0:T(8,128)(2,1)} %get-tuple-element.42), calls=%async_computation.3 | async-start | bytes 786432 | tf_op jit(solution)/shard_map/all_to_all | solution.py:341
